TPU v7x, 256 devices: a whole 4x4x8 slice. The times are simulated.
256 devices in a mesh: gx: 16 (over z, core), gy: 16 (over y, x).
Axes of the slice: x: 4, y: 4, z: 8, core: 2. Of those that a mesh axis runs over, the one named last changes fastest.
Arguments:
- velocity: float32 [2, 2048, 2048], P(None, 'gy', 'gx'), may hold values from -6 to 6
- wind_stress: float32 [2, 2048, 2048], P(None, 'gy', 'gx'), may hold values from -6 to 6
- thickness: float32 [2048, 2048], P('gy', 'gx'), may hold values from 0.3 to 3
- ice_mask: int32 [2048, 2048], P('gy', 'gx'), may hold values from 0 to 1
- land_mask: int32 [2048, 2048], P('gy', 'gx'), may hold values from 0 to 1
Outputs:
- velocity_out: float32 [2, 2048, 2048], P(None, 'gy', 'gx')
All inputs are finite; a program needn't handle non-finite values.
Results may differ from a plain program's by a relative error of at most 0.0012.
Values sent between devices are 32-bit elements; how exact they have to be, the bound alone decides.
No kernel may reach another device: no remote copies, remote signals or barrier semaphores. Data moves between devices by JAX's collectives and lax.ppermute only.
A program may use at most 64 MiB of HBM per device.

v0:
```python
import jax
import jax.numpy as jnp
from jax import lax
from jax.experimental import pallas as pl
from jax.experimental.pallas import tpu as pltpu
from jax.sharding import PartitionSpec as P

CORIOLIS = 1.0
DELTA_MIN = 0.25
WIND_GAIN = 0.2

N = 128
K = 16
TOP = 16
ROWS = N + 2 * TOP
CELLS = float(N * N)
WEAK = 1.0 / (16.0 * CELLS)
PRESS = CELLS ** (-0.25)
DRIVE = WIND_GAIN * CELLS ** (-0.75)
F32 = jnp.float32


def lanes(rows):
    return lax.broadcasted_iota(jnp.int32, (rows, N), 1)


def sublanes(rows):
    return lax.broadcasted_iota(jnp.int32, (rows, N), 0)


def east(own, side):
    a, b = pltpu.roll(own, N - 1, 1), pltpu.roll(side, N - 1, 1)
    last = lanes(own.shape[0]) == N - 1
    return jnp.where(last, b, a), jnp.where(last, a, b)


def west(own, side):
    a, b = pltpu.roll(own, 1, 1), pltpu.roll(side, 1, 1)
    first = lanes(own.shape[0]) == 0
    return jnp.where(first, b, a), jnp.where(first, a, b)


def pick(flag, rows, a, b):
    return jnp.where(jnp.broadcast_to(flag, (rows, N)), a, b)


def pack_columns(vel, wind, thick, ice, land, send_a, send_b, turn):
    live = (ice[...] * (1 - land[...])).astype(F32)
    lane = lanes(N)
    mixed = jnp.where(lane < 36, pltpu.roll(live, 32, 1), vel[0])
    mixed = jnp.where(lane < 28, pltpu.roll(wind[1], 24, 1), mixed)
    mixed = jnp.where(lane < 20, pltpu.roll(thick[...], 16, 1), mixed)
    mixed = jnp.where(lane < 12, pltpu.roll(vel[1], 8, 1), mixed)
    mixed = jnp.where(lane < 4, vel[0], mixed)
    turn[...] = mixed.T
    left = [turn[0:4], turn[8:12], turn[16:20], turn[24:26], turn[32:34]]
    right = [turn[124:128], turn[4:8], turn[12:16], turn[22:24], turn[30:32]]
    even = lax.rem(lax.axis_index("gx"), 2) == 0
    at = 0
    for a, b in zip(left, right):
        n = a.shape[0]
        send_a[at : at + n] = pick(even, n, b, a)
        send_b[at : at + n] = pick(even, n, a, b)
        at += n


def side_columns(got_a, got_b, turn):
    even = lax.rem(lax.axis_index("gx"), 2) == 0
    turn[...] = jnp.zeros((N, N), F32)
    places = ((0, 4, 0, 124), (4, 4, 8, 4), (8, 4, 16, 12), (12, 2, 24, 22), (14, 2, 32, 30))
    for at, n, low, high in places:
        a, b = got_a[at : at + n], got_b[at : at + n]
        turn[low : low + n] = pick(even, n, a, b)
        turn[high : high + n] = pick(even, n, b, a)
    return turn[...].T


def side_field(mixed, slot):
    lane = lanes(N)
    moved = mixed if slot == 0 else pltpu.roll(mixed, N - 8 * slot, 1)
    return jnp.where((lane < 4) | (lane >= 124), moved, 0.0)


def pack_rows(vel, thick, got_a, got_b, send_a, send_b, turn, work):
    mixed = side_columns(got_a, got_b, turn)
    even = lax.rem(lax.axis_index("gy"), 2) == 0
    for k in range(3):
        turn[...] = side_field(mixed, k)
        own = vel.at[k] if k < 2 else thick
        for tile, source in ((0, own), (1, turn)):
            low, high = source[0:2], source[126:128]
            at = 8 * tile + 2 * k
            send_a[at : at + 2] = pick(even, 2, high, low)
            send_b[at : at + 2] = pick(even, 2, low, high)
    for tile in (0, 1):
        send_a[8 * tile + 6 : 8 * tile + 8] = jnp.zeros((2, N), F32)
        send_b[8 * tile + 6 : 8 * tile + 8] = jnp.zeros((2, N), F32)


def root_viscosity(su, sv, st, sh):
    for at in range(TOP - 8, TOP + N + 8, 8):
        here = slice(at, at + 8)
        up, down = slice(at + 1, at + 9), slice(at - 1, at + 7)
        ue, uw = east(su[0, here], su[1, here]), west(su[0, here], su[1, here])
        ve, vw = east(sv[0, here], sv[1, here]), west(sv[0, here], sv[1, here])
        for t in (0, 1):
            strain_xx = 0.5 * (ue[t] - uw[t])
            strain_yy = 0.5 * (sv[t, up] - sv[t, down])
            shear = 0.25 * (su[t, up] - su[t, down] + (ve[t] - vw[t]))
            delta2 = (
                1.25 * (strain_xx * strain_xx + strain_yy * strain_yy)
                + shear * shear
                + 1.5 * strain_xx * strain_yy
            )
            sh[t, here] = jnp.sqrt(st[t, here] / (2.0 * jnp.sqrt(delta2 + DELTA_MIN * DELTA_MIN)))


def systems(su, sv, st, sh, wx, wy, live, tiles, put_u, put_v):
    for at in range(TOP, TOP + N, 8):
        here = slice(at, at + 8)
        up, down = slice(at + 1, at + 9), slice(at - 1, at + 7)
        cell = slice(at - TOP, at - TOP + 8)
        he, hw = east(sh[0, here], sh[1, here]), west(sh[0, here], sh[1, here])
        ve, vw = east(sv[0, here], sv[1, here]), west(sv[0, here], sv[1, here])
        te, tw = east(st[0, here], st[1, here]), west(st[0, here], st[1, here])
        for t in tiles:
            h, thick = sh[t, here], st[t, here]
            e_edge, w_edge = h * he[t], h * hw[t]
            n_edge, s_edge = h * sh[t, up], h * sh[t, down]
            mass = WEAK * thick
            alive = live(t, cell) > 0.5
            if t == 0:
                extra = mass + WEAK * (n_edge + s_edge)
                right = (
                    mass * su[0, here]
                    + DRIVE * wx(cell)
                    + CORIOLIS * mass * sv[0, here]
                    + WEAK * (n_edge * su[0, up] + s_edge * su[0, down])
                    - 0.5 * PRESS * (te[0] - tw[0])
                )
                scale = 1.0 / (extra + e_edge + w_edge)
                put_u(
                    cell,
                    jnp.where(alive, w_edge * scale, 0.0),
                    jnp.where(alive, e_edge * scale, 0.0),
                    jnp.where(alive, extra * scale, 1.0),
                    jnp.where(alive, right * scale, 0.0),
                )
            extra = mass + WEAK * (e_edge + w_edge)
            right = (
                mass * sv[t, here]
                + DRIVE * wy(t, cell)
                + WEAK * (e_edge * ve[t] + w_edge * vw[t])
                - 0.5 * PRESS * (st[t, up] - st[t, down])
            )
            scale = 1.0 / jnp.where(alive, extra + n_edge + s_edge, 1.0)
            put_v(
                t,
                cell,
                jnp.where(alive, s_edge * scale, 0.0),
                jnp.where(alive, n_edge * scale, 0.0),
                jnp.where(alive, extra * scale, 1.0),
                jnp.where(alive, right * scale, 0.0),
                jnp.where(alive, CORIOLIS * mass * scale, 0.0),
            )


def set_rims(bands):
    one, zero = jnp.ones((8, N), F32), jnp.zeros((8, N), F32)
    for half in (0, 1):
        for k in range(4):
            bands[half, k, 0:8] = one if k == 0 else zero
            bands[half, k, 8 + N : 16 + N] = one if k == 1 else zero


def set_band(bands, k, at, value):
    if at + value.shape[0] == N:
        own = sublanes(value.shape[0]) == value.shape[0] - 1
        value = jnp.where(own, 1.0 if k == 1 else 0.0, value)
    bands[0, k, 8 + at : 8 + at + value.shape[0]] = value


def reduce_piece(bands, last, out):
    half, s = 0, 1
    while s < N:
        final = 2 * s >= N
        for at in range(0, N, 8):
            here = slice(8 + at, 16 + at)
            l, u, e, r = (bands[half, k, here] for k in range(4))
            ll, uu, ee, rr = l, u, e, r
            if s < 8 or at >= s:
                low = slice(8 + at - s, 16 + at - s)
                ll = l * bands[half, 0, low]
                ee = ee + l * bands[half, 2, low]
                rr = rr + l * bands[half, 3, low]
            if s < 8 or at + s < N:
                high = slice(8 + at + s, 16 + at + s)
                uu = u * bands[half, 1, high]
                ee = ee + u * bands[half, 2, high]
                rr = rr + u * bands[half, 3, high]
            q = 1.0 / (ll + uu + ee)
            for k, x in enumerate((ll, uu, ee, rr)):
                if final:
                    out(k, at, x * q)
                if not final or at in (0, N - 8):
                    bands[1 - half, k, here] = x * q
        half, s = 1 - half, 2 * s
    row = lambda k, i: bands[half, k, 8 + i : 9 + i]
    lo, uo, eo, ro = last
    lq, uq, eq, rq = (row(k, N - 2) for k in range(4))
    q = 1.0 / (uo + eo + lo * (lq + eq))
    coupling = [row(k, 0) for k in range(4)]
    coupling += [lo * lq * q, uo * q, (eo + lo * eq) * q, (ro + lo * rq) * q]
    second = [row(k, 1) for k in (0, 1, 3)]
    return coupling, second, [lq, uq, rq]


def solve_pieces(got, width, base, me, rowed, halo=None):
    take = lambda k: got[pl.ds(base + k, K, width), :]
    fl, fu, fe, fr, zl, zu, ze, zr = (take(k) for k in range(8))
    nxt = lambda a: pltpu.roll(a, K - 1, 0)
    fe = nxt(fe)
    uu, ee, rr = zu * nxt(fu), ze + zu * fe, zr + zu * nxt(fr)
    q = 1.0 / (zl + ee + uu)
    l, u, e, r = zl * q, uu * q, ee * q, rr * q
    s = 1
    while s < K:
        low = lambda a: pltpu.roll(a, s, 0)
        high = lambda a: pltpu.roll(a, K - s, 0)
        ee = e + l * low(e) + u * high(e)
        rr = r + l * low(r) + u * high(r)
        ll, uu = l * low(l), u * high(u)
        q = 1.0 / (ll + uu + ee)
        l, u, e, r = ll * q, uu * q, ee * q, rr * q
        s *= 2
    rowed[0:K] = jnp.zeros((K, N), F32)
    rowed[K : 2 * K] = r
    rowed[2 * K : 3 * K] = jnp.zeros((K, N), F32)
    before, own = rowed[pl.ds(K - 1 + me, 1), :], rowed[pl.ds(K + me, 1), :]
    if halo is None:
        return before, own
    before2, after = rowed[pl.ds(K - 2 + me, 1), :], rowed[pl.ds(K + 1 + me, 1), :]
    up = jnp.minimum(me + 1, K - 1) * width
    down = jnp.maximum(me - 1, 0) * width
    has_up = jnp.broadcast_to(me < K - 1, (1, N))
    has_down = jnp.broadcast_to(me > 0, (1, N))
    row = lambda at, k: got[pl.ds(at + k, 1), :]
    first = row(up, base + 3) + row(up, base) * own + row(up, base + 1) * after
    first = jnp.where(has_up, first, 0.0)
    second = row(up, halo + 2) + row(up, halo) * own + row(up, halo + 1) * after
    second = jnp.where(has_up, second, 0.0)
    ahead = row(down, halo + 2) + row(down, halo) * before2 + row(down, halo + 1) * before
    ahead = jnp.where(has_down, ahead, 0.0)
    return before, own, ahead, first, second


def spread(dest, me, common, forward, backward, width):
    for d in range(K):
        at = d * width
        dest[at : at + 8 * len(common)] = jnp.concatenate(common, 0) if len(common) > 1 else common[0]
        if forward is not None:
            dest[at + width - 8 : at + width] = pick(me < d, 8, forward, backward)


def tile_of(rows, pad):
    for k, row in enumerate(rows):
        pad[k : k + 1] = row
    return pad[...]


def first_u(vel, wind, thick, ice, land, ca, cb, ra, rb, send, pl_, pu_, pr_, vsys, sth, su, sv, st, sh, turn, tall, bands, pad):
    mixed = side_columns(ca, cb, turn)
    even = lax.rem(lax.axis_index("gy"), 2) == 0
    zero = jnp.zeros((TOP, N), F32)
    for k, s in enumerate((su, sv, st)):
        own = vel.at[k] if k < 2 else thick
        for t in (0, 1):
            s[t, 0:TOP] = zero
            s[t, TOP + N :] = zero
            s[t, TOP : TOP + N] = own[...] if t == 0 else side_field(mixed, k)
            at = 8 * t + 2 * k
            a, b = ra[at : at + 2], rb[at : at + 2]
            s[t, TOP + N : TOP + N + 2] = pick(even, 2, a, b)
            s[t, TOP - 2 : TOP] = pick(even, 2, b, a)
    tall[0] = side_field(mixed, 3)
    tall[1] = side_field(mixed, 4)
    root_viscosity(su, sv, st, sh)

    def live(t, cell):
        if t == 0:
            return (ice[cell] * (1 - land[cell])).astype(F32)
        return tall[1, cell]

    def wy(t, cell):
        return wind[1, cell] if t == 0 else tall[0, cell]

    def put_u(cell, *values):
        for k, x in enumerate(values):
            tall[2 + k, cell] = x

    def put_v(t, cell, *values):
        for k, x in enumerate(values):
            vsys[k, t, cell] = x

    systems(su, sv, st, sh, lambda cell: wind[0, cell], wy, live, (0, 1), put_u, put_v)
    for t in (0, 1):
        sth[t] = st[t]
    last = []
    for k in range(4):
        turned = tall[2 + k].T
        set_band(bands, k, 0, turned)
        last.append(turned[N - 1 :])
    set_rims(bands)
    outs = {0: pl_, 1: pu_, 3: pr_}

    def out(k, at, x):
        if k != 2:
            outs[k][at : at + 8] = x

    main, second, ahead = reduce_piece(bands, last, out)
    me = lax.axis_index("gx")
    common = tile_of(main, pad)
    pad[...] = jnp.zeros((8, N), F32)
    forward = tile_of(ahead, pad)
    backward = tile_of(second, pad)
    spread(send, me, [common], forward, backward, 16)


def load_v(bands, vsys, t, speed):
    last = []
    for k in range(4):
        x = vsys[k, t]
        if k == 3:
            x = x - vsys[4, t] * speed
        set_band(bands, k, 0, x)
        last.append(x[N - 1 :])
    set_rims(bands)
    return last


def first_v(got, pl_, pu_, pr_, vsys, send, u_new, vp, turn, bands, pad, rowed):
    me = lax.axis_index("gx")
    before, own, ahead, first, second = solve_pieces(got, 16, 0, me, rowed, 8)
    turn[...] = pr_[...] + pl_[...] * before + pu_[...] * own
    u_new[0] = turn[...].T
    turn[...] = jnp.zeros((N, N), F32)
    turn[0:1] = first
    turn[1:2] = second
    turn[N - 2 : N - 1] = ahead
    turn[N - 1 : N] = before
    u_new[1] = turn[...].T
    mains = []
    for t in (0, 1):
        last = load_v(bands, vsys, t, u_new[t])

        def out(k, at, x):
            if k != 2:
                vp[min(k, 2), t, at : at + 8] = x

        main, second, ahead = reduce_piece(bands, last, out)
        mains.append(tile_of(main, pad))
        if t == 0:
            extras = (ahead, second)
    pad[...] = jnp.zeros((8, N), F32)
    last_rows = [u_new[0, N - 2 : N - 1], u_new[0, N - 1 : N], u_new[1, N - 1 : N]]
    first_rows = [u_new[0, 1:2], u_new[0, 0:1], u_new[1, 0:1]]
    forward = tile_of(extras[0] + last_rows, pad)
    backward = tile_of(extras[1] + first_rows, pad)
    spread(send, lax.axis_index("gy"), mains, forward, backward, 24)


def second_u(got, vp, u_new, sth, wind, ice, land, send, pl_, pu_, pr_, vsys, su, sv, sh, tall, bands, pad, rowed):
    me = lax.axis_index("gy")
    up = jnp.minimum(me + 1, K - 1) * 24
    down = jnp.maximum(me - 1, 0) * 24
    has_up = jnp.broadcast_to(me < K - 1, (1, N))
    has_down = jnp.broadcast_to(me > 0, (1, N))
    zero = jnp.zeros((TOP, N), F32)
    for t in (0, 1):
        before, own, ahead, first, second = solve_pieces(got, 24, 8 * t, me, rowed, 16)
        for s in (su, sv):
            s[t, 0:TOP] = zero
            s[t, TOP + N :] = zero
        sv[t, TOP : TOP + N] = vp[2, t] + vp[0, t] * before + vp[1, t] * own
        sv[t, TOP - 1 : TOP] = before
        sv[t, TOP + N : TOP + N + 1] = first
        su[t, TOP : TOP + N] = u_new[t]
        near = 20 if t == 0 else 21
        row = lambda at, k: got[pl.ds(at + k, 1), :]
        su[t, TOP - 1 : TOP] = jnp.where(has_down, row(down, near), 0.0)
        su[t, TOP + N : TOP + N + 1] = jnp.where(has_up, row(up, near), 0.0)
        if t == 0:
            sv[0, TOP - 2 : TOP - 1] = ahead
            sv[0, TOP + N + 1 : TOP + N + 2] = second
            su[0, TOP - 2 : TOP - 1] = jnp.where(has_down, row(down, 19), 0.0)
            su[0, TOP + N + 1 : TOP + N + 2] = jnp.where(has_up, row(up, 19), 0.0)
    root_viscosity(su, sv, sth, sh)

    def live(t, cell):
        return (ice[cell] * (1 - land[cell])).astype(F32)

    def put_u(cell, *values):
        for k, x in enumerate(values):
            tall[k, cell] = x

    def put_v(t, cell, *values):
        for k, x in enumerate(values):
            vsys[k, t, cell] = x

    systems(su, sv, sth, sh, lambda cell: wind[0, cell], lambda t, cell: wind[1, cell], live, (0,), put_u, put_v)
    last = []
    for k in range(4):
        turned = tall[k].T
        set_band(bands, k, 0, turned)
        last.append(turned[N - 1 :])
    set_rims(bands)
    outs = {0: pl_, 1: pu_, 3: pr_}

    def out(k, at, x):
        if k != 2:
            outs[k][at : at + 8] = x

    main, _, _ = reduce_piece(bands, last, out)
    spread(send, lax.axis_index("gx"), [tile_of(main, pad)], None, None, 8)


def second_v(got, pl_, pu_, pr_, vsys, send, u_new, vp, turn, bands, pad, rowed):
    before, own = solve_pieces(got, 8, 0, lax.axis_index("gx"), rowed)
    turn[...] = pr_[...] + pl_[...] * before + pu_[...] * own
    u_new[...] = turn[...].T
    last = load_v(bands, vsys, 0, u_new[...])

    def out(k, at, x):
        if k != 2:
            vp[min(k, 2), at : at + 8] = x

    main, _, _ = reduce_piece(bands, last, out)
    spread(send, lax.axis_index("gy"), [tile_of(main, pad)], None, None, 8)


def finish(got, vp, u_new, out, rowed):
    before, own = solve_pieces(got, 8, 0, lax.axis_index("gy"), rowed)
    out[0] = u_new[...]
    out[1] = vp[2] + vp[0] * before + vp[1] * own


def call(kernel, outs, scratch, *args):
    vmem = pl.BlockSpec(memory_space=pltpu.VMEM)
    shapes = [jax.ShapeDtypeStruct(s, F32) for s in outs]
    return pl.pallas_call(
        kernel,
        out_shape=shapes,
        in_specs=[vmem] * len(args),
        out_specs=[vmem] * len(outs),
        scratch_shapes=[pltpu.VMEM(s, F32) for s in scratch],
    )(*args)


def neighbours(a, b, axis):
    inner = [(i, i ^ 1) for i in range(K)]
    outer = [p for i in range(1, K - 1, 2) for p in ((i, i + 1), (i + 1, i))]
    return lax.ppermute(a, axis, inner), lax.ppermute(b, axis, outer)


def share(rows, axis):
    width = rows.shape[0] // K
    moved = lax.all_to_all(rows.reshape(K, width, N), axis, 0, 0, tiled=True)
    return moved.reshape(K * width, N)


def on_device(velocity, wind, thick, ice, land):
    square, halves, rim = (N, N), (2, N, N), (2, ROWS, N)
    bands, pad, rowed = (2, 4, N + 16, N), (8, N), (3 * K, N)
    a, b = call(pack_columns, [(16, N)] * 2, [square], velocity, wind, thick, ice, land)
    ca, cb = neighbours(a, b, "gx")
    a, b = call(pack_rows, [(16, N)] * 2, [square, pad], velocity, thick, ca, cb)
    ra, rb = neighbours(a, b, "gy")
    send, l, u, r, vsys, sth = call(
        first_u,
        [(K * 16, N), square, square, square, (5,) + halves, rim],
        [rim] * 4 + [square, (6, N, N), bands, pad],
        velocity, wind, thick, ice, land, ca, cb, ra, rb,
    )
    got = share(send, "gx")
    send, u_new, vp = call(
        first_v,
        [(K * 24, N), halves, (3,) + halves],
        [square, bands, pad, rowed],
        got, l, u, r, vsys,
    )
    got = share(send, "gy")
    send, l, u, r, vsys = call(
        second_u,
        [(K * 8, N), square, square, square, (5, 1, N, N)],
        [rim] * 3 + [(4, N, N), bands, pad, rowed],
        got, vp, u_new, sth, wind, ice, land,
    )
    got = share(send, "gx")
    send, u_new, vp = call(
        second_v,
        [(K * 8, N), square, (3, N, N)],
        [square, bands, pad, rowed],
        got, l, u, r, vsys,
    )
    got = share(send, "gy")
    (out,) = call(finish, [halves], [rowed], got, vp, u_new)
    return out


def solution(mesh):
    field = P(None, "gy", "gx")
    flat = P("gy", "gx")
    return jax.shard_map(
        on_device,
        mesh=mesh,
        in_specs=(field, field, flat, flat, flat),
        out_specs=field,
        check_vma=False,
    )
```

profile of v0, /device:TPU:1, one launch (start us, length us, event | category | flops | bytes accessed | tf_op | source)
XLA Modules:
  0.0 89.5 jit_solution(15695882253613348935)
XLA Ops:
  0.0 1.8 %shard_map.55 = (f32[16,128]{1,0:T(8,128)}, f32[16,128]{1,0:T(8,128)}) custom-call(f32[2,128,128]{2,1,0:T(8,128)} %vel.5, f32[2,128,128]{2,1,0:T(8,128)} %wind.5, f32[128,128]{1,0:T(8,128)} %thick.5, s32[128,128]{1,0:T(8,128)} %ice.5, s32[128,128]{1,0:T(8,128)} %land.5), custom_call_target="tpu_custom_call" | custom-call | tf_op jit(solution)/shard_map/pallas_call | solution.py:450
  1.8 3.2 %collective-permute-start = (f32[16,128]{1,0:T(8,128)}, f32[16,128]{1,0:T(8,128)S(1)}, u32[]{:S(2)}, u32[]{:S(2)}) collective-permute-start(f32[16,128]{1,0:T(8,128)} %get-tuple-element.26), channel_id=1, source_target_pairs={{0,16},{16,0},{32,48},{48,32},{64,80},{80,64},{96,112},{112,96},{1... | collective-permute-start | bytes 24584 | tf_op jit(solution)/shard_map/ppermute | solution.py:462
  5.0 1.9 %collective-permute-start.1 = (f32[16,128]{1,0:T(8,128)}, f32[16,128]{1,0:T(8,128)S(1)}, u32[]{:S(2)}, u32[]{:S(2)}) collective-permute-start(f32[16,128]{1,0:T(8,128)} %get-tuple-element.27), channel_id=1, source_target_pairs={{16,32},{32,16},{48,64},{64,48},{80,96},{96,80},{112,128},{128,112... | collective-permute-start | bytes 24584 | tf_op jit(solution)/shard_map/ppermute | solution.py:462
  7.0 0.0 collective-permute-done.got_a.ca
  7.0 0.0 copy-start
  7.0 3.2 %collective-permute-done.1.got_b.cb = f32[16,128]{1,0:T(8,128)S(1)} collective-permute-done((f32[16,128]{1,0:T(8,128)}, f32[16,128]{1,0:T(8,128)S(1)}, u32[]{:S(2)}, u32[]{:S(2)}) %collective-permute-start.1) | collective-permute-done | bytes 8224 | tf_op jit(solution)/shard_map/ppermute | solution.py:462
  10.2 0.0 copy-done
  10.2 0.6 copy-done.1
  10.8 1.8 %shard_map.56 = (f32[16,128]{1,0:T(8,128)}, f32[16,128]{1,0:T(8,128)}) custom-call(f32[2,128,128]{2,1,0:T(8,128)} %vel.5, f32[128,128]{1,0:T(8,128)} %thick.5, f32[16,128]{1,0:T(8,128)} %copy-done, f32[16,128]{1,0:T(8,128)} %copy-done.1), custom_call_target="tpu_custom_call" | custom-call | tf_op jit(solution)/shard_map/pallas_call | solution.py:450
  12.6 0.0 collective-permute-start.2
  12.6 0.7 collective-permute-start.3
  13.2 2.1 %collective-permute-done.2.ra = f32[16,128]{1,0:T(8,128)S(1)} collective-permute-done((f32[16,128]{1,0:T(8,128)}, f32[16,128]{1,0:T(8,128)S(1)}, u32[]{:S(2)}, u32[]{:S(2)}) %collective-permute-start.2) | collective-permute-done | bytes 8224 | tf_op jit(solution)/shard_map/ppermute | solution.py:462
  15.3 0.0 collective-permute-done.3.rb
  15.3 0.6 copy-done.2
  15.9 0.6 copy-done.3
  16.5 3.2 %shard_map.57 = (f32[256,128]{1,0:T(8,128)}, f32[128,128]{1,0:T(8,128)}, f32[128,128]{1,0:T(8,128)}, f32[128,128]{1,0:T(8,128)}, f32[5,2,128,128]{3,2,1,0:T(8,128)}, /*index=5*/f32[2,160,128]{2,1,0:T(8,128)}) custom-call(f32[2,128,128]{2,1,0:T(8,128)} %vel.5, f32[2,128,128]{2,1,0:T(8,128)} %wind.5, f32[128,128]{1,0:T(8,128)} %thick.5, s32[128,128]{1,0:T(8,128)} %ice.5, ...), custom_call_target="tpu_custom_call" | custom-call | tf_op jit(solution)/shard_map/pallas_call | solution.py:450
  19.6 18.1 %all_to_all.20 = f32[16,16,128]{2,1,0:T(8,128)} all-to-all(f32[16,16,128]{2,1,0:T(8,128)} %bitcast.13), channel_id=1, replica_groups=mesh['gx'=16,'gy'=16] {'gx'}, dimensions={0} | all-to-all | bytes 262144 | tf_op jit(solution)/shard_map/all_to_all | solution.py:467
  37.8 2.7 %shard_map.58 = (f32[384,128]{1,0:T(8,128)}, f32[2,128,128]{2,1,0:T(8,128)}, f32[3,2,128,128]{3,2,1,0:T(8,128)}) custom-call(f32[256,128]{1,0:T(8,128)} %bitcast.9, f32[128,128]{1,0:T(8,128)} %get-tuple-element.31.pl_, f32[128,128]{1,0:T(8,128)} %get-tuple-element.32.pu_, f32[128,128]{1,0:T(8,128)} %get-tuple-element.33.pr_, ...), custom_call_target="tpu_custom_call" | custom-call | tf_op jit(solution)/shard_map/pallas_call | solution.py:450
  40.5 18.7 %all_to_all.21 = f32[16,24,128]{2,1,0:T(8,128)} all-to-all(f32[16,24,128]{2,1,0:T(8,128)} %bitcast.12), channel_id=1, replica_groups=mesh['gx'=16,'gy'=16] {'gy'}, dimensions={0} | all-to-all | bytes 393216 | tf_op jit(solution)/shard_map/all_to_all | solution.py:467
  59.2 3.0 %shard_map.59 = (f32[128,128]{1,0:T(8,128)}, f32[128,128]{1,0:T(8,128)}, f32[128,128]{1,0:T(8,128)}, f32[128,128]{1,0:T(8,128)}, f32[5,1,128,128]{3,2,1,0:T(8,128)}) custom-call(f32[384,128]{1,0:T(8,128)} %bitcast.8, f32[3,2,128,128]{3,2,1,0:T(8,128)} %get-tuple-element.36.vp, f32[2,128,128]{2,1,0:T(8,128)} %get-tuple-element.37.u_new, ...), custom_call_target="tpu_custom_call" | custom-call | tf_op jit(solution)/shard_map/pallas_call | solution.py:450
  62.2 12.8 %all_to_all.22 = f32[16,8,128]{2,1,0:T(8,128)} all-to-all(f32[16,8,128]{2,1,0:T(8,128)} %bitcast.14), channel_id=1, replica_groups=mesh['gx'=16,'gy'=16] {'gx'}, dimensions={0} | all-to-all | bytes 131072 | tf_op jit(solution)/shard_map/all_to_all | solution.py:467
  75.0 2.2 %shard_map.60 = (f32[128,128]{1,0:T(8,128)}, f32[128,128]{1,0:T(8,128)}, f32[3,128,128]{2,1,0:T(8,128)}) custom-call(f32[128,128]{1,0:T(8,128)} %bitcast.10, f32[128,128]{1,0:T(8,128)} %get-tuple-element.40.pl_, f32[128,128]{1,0:T(8,128)} %get-tuple-element.41.pu_, f32[128,128]{1,0:T(8,128)} %get-tuple-element.42.pr_, f32[5,1,128,128]{3,2,1,0:T(8,128)} %get-tuple-element.43.vsys), custom_call_target="tpu_custom_call" | custom-call | tf_op jit(solution)/shard_map/pallas_call | solution.py:450
  77.2 10.6 %all_to_all.23 = f32[16,8,128]{2,1,0:T(8,128)} all-to-all(f32[16,8,128]{2,1,0:T(8,128)} %bitcast.15), channel_id=1, replica_groups=mesh['gx'=16,'gy'=16] {'gy'}, dimensions={0} | all-to-all | bytes 131072 | tf_op jit(solution)/shard_map/all_to_all | solution.py:467
  87.8 1.7 %shard_map.61 = f32[2,128,128]{2,1,0:T(8,128)} custom-call(f32[128,128]{1,0:T(8,128)} %bitcast.11, f32[3,128,128]{2,1,0:T(8,128)} %get-tuple-element.45.vp, f32[128,128]{1,0:T(8,128)} %get-tuple-element.46.u_new), custom_call_target="tpu_custom_call" | custom-call | tf_op jit(solution)/shard_map/pallas_call | solution.py:450
  (3 shorter events, 0.0 us)
Async XLA Ops:
  1.8 5.1 %collective-permute-start = (f32[16,128]{1,0:T(8,128)}, f32[16,128]{1,0:T(8,128)S(1)}, u32[]{:S(2)}, u32[]{:S(2)}) collective-permute-start(f32[16,128]{1,0:T(8,128)} %get-tuple-element.26), channel_id=1, source_target_pairs={{0,16},{16,0},{32,48},{48,32},{64,80},{80,64},{96,112},{112,96},{1... | collective-permute-start | bytes 24584 | tf_op jit(solution)/shard_map/ppermute | solution.py:462
  5.0 5.2 %collective-permute-start.1 = (f32[16,128]{1,0:T(8,128)}, f32[16,128]{1,0:T(8,128)S(1)}, u32[]{:S(2)}, u32[]{:S(2)}) collective-permute-start(f32[16,128]{1,0:T(8,128)} %get-tuple-element.27), channel_id=1, source_target_pairs={{16,32},{32,16},{48,64},{64,48},{80,96},{96,80},{112,128},{128,112... | collective-permute-start | bytes 24584 | tf_op jit(solution)/shard_map/ppermute | solution.py:462
  7.0 3.2 %copy-start = (f32[16,128]{1,0:T(8,128)}, f32[16,128]{1,0:T(8,128)S(1)}, u32[]{:S(2)}) copy-start(f32[16,128]{1,0:T(8,128)S(1)} %collective-permute-done.got_a.ca) | copy-start | bytes 24580
  10.2 0.6 copy-start.1
  12.6 2.7 %collective-permute-start.2 = (f32[16,128]{1,0:T(8,128)}, f32[16,128]{1,0:T(8,128)S(1)}, u32[]{:S(2)}, u32[]{:S(2)}) collective-permute-start(f32[16,128]{1,0:T(8,128)} %get-tuple-element.28), channel_id=1, source_target_pairs={{0,1},{1,0},{2,3},{3,2},{4,5},{5,4},{6,7},{7,6},{8,9},{9,8},{10,11... | collective-permute-start | bytes 24584 | tf_op jit(solution)/shard_map/ppermute | solution.py:462
  12.6 2.7 %collective-permute-start.3 = (f32[16,128]{1,0:T(8,128)}, f32[16,128]{1,0:T(8,128)S(1)}, u32[]{:S(2)}, u32[]{:S(2)}) collective-permute-start(f32[16,128]{1,0:T(8,128)} %get-tuple-element.29), channel_id=1, source_target_pairs={{1,2},{2,1},{3,4},{4,3},{5,6},{6,5},{7,8},{8,7},{9,10},{10,9},{11,... | collective-permute-start | bytes 24584 | tf_op jit(solution)/shard_map/ppermute | solution.py:462
  15.3 0.6 copy-start.2
  15.9 0.6 copy-start.3
where the time goes:
time: 90.1 us; the launch traced here: 89.5 us
  blocking collectives  60.3 us (67%)
  Pallas kernels  16.4 us (18%)
  starting transfers between devices  5.76 us (6%)
  waiting for transfers between devices  5.29 us (6%)
  local copies, waits for them, and re-layouts  1.79 us (2%)
    all_to_all x4, blocking collectives, share(): moved = lax.all_to_all(rows.reshape(K, width, N), axis, 0, 0, tiled=True)  60.3 us
    pallas_call x7, Pallas kernels, call(): pl.pallas_call(kernel, out_shape=shapes, in_specs=[vmem] * len(args), out...  16.4 us
    ppermute x4, starting transfers between devices, neighbours(): return (lax.ppermute(a, axis, inner), lax.ppermute(b, axis, outer))  5.76 us
    ppermute x4, waiting for transfers between devices, neighbours(): return (lax.ppermute(a, axis, inner), lax.ppermute(b, axis, outer))  5.29 us
  transfers between devices with their start and end apart: 4, of which 2 were waited for; matrix products, arithmetic and copies ran while one was open for 0% of the time, Pallas kernels for 0%

commit v1 on v0

--- a/solution.py
+++ b/solution.py
@@ -453,6 +453,7 @@
         in_specs=[vmem] * len(args),
         out_specs=[vmem] * len(outs),
         scratch_shapes=[pltpu.VMEM(s, F32) for s in scratch],
+        compiler_params=pltpu.CompilerParams(vmem_limit_bytes=8 * 1024 * 1024),
     )(*args)
 
 

time: 90.1 us -> 77.6 us (0.86)
  Pallas kernels: 16.4 us -> 4.45 us
  blocking collectives: 60.3 us -> 57.5 us
  local copies, waits for them, and re-layouts: 1.79 us -> 4.34 us
    pallas_call x7, Pallas kernels: 16.4 us -> 4.45 us  [call(): pl.pallas_call(kernel, out_shape=shapes, in_specs=[vmem] * len(args), out...]
    all_to_all x4, blocking collectives: 60.3 us -> 57.5 us  [share(): moved = lax.all_to_all(rows.reshape(K, width, N), axis, 0, 0, tiled=True)]
    unnamed x8 -> x16, local copies, waits for them, and re-layouts: 1.79 us -> 4.34 us
where the time goes in v1:
time: 77.6 us; the launch traced here: 77.1 us
  blocking collectives  57.5 us (74%)
  starting transfers between devices  5.95 us (8%)
  waiting for transfers between devices  4.85 us (6%)
  Pallas kernels  4.45 us (6%)
  local copies, waits for them, and re-layouts  4.34 us (6%)
    all_to_all x4, blocking collectives, share(): moved = lax.all_to_all(rows.reshape(K, width, N), axis, 0, 0, tiled=True)  57.5 us
    ppermute x4, starting transfers between devices, neighbours(): return (lax.ppermute(a, axis, inner), lax.ppermute(b, axis, outer))  5.95 us
    ppermute x4, waiting for transfers between devices, neighbours(): return (lax.ppermute(a, axis, inner), lax.ppermute(b, axis, outer))  4.85 us
    pallas_call x7, Pallas kernels, call(): pl.pallas_call(kernel, out_shape=shapes, in_specs=[vmem] * len(args), out...  4.45 us
    unnamed x16, local copies, waits for them, and re-layouts  4.34 us
  transfers between devices with their start and end apart: 4, of which 2 were waited for; matrix products, arithmetic and copies ran while one was open for 0% of the time, Pallas kernels for 0%

profile of v1, /device:TPU:1, one launch (start us, length us, event | category | flops | bytes accessed | tf_op | source)
XLA Modules:
  0.0 77.1 jit_solution(12276562673880812937)
XLA Ops:
  0.0 0.9 %copy-done = f32[2,128,128]{2,1,0:T(8,128)S(1)} copy-done((f32[2,128,128]{2,1,0:T(8,128)S(1)}, f32[2,128,128]{2,1,0:T(8,128)}, u32[]{:S(2)}) %copy-start) | copy-done | bytes 131096
  0.9 0.9 %copy-done.2 = f32[2,128,128]{2,1,0:T(8,128)S(1)} copy-done((f32[2,128,128]{2,1,0:T(8,128)S(1)}, f32[2,128,128]{2,1,0:T(8,128)}, u32[]{:S(2)}) %copy-start.2) | copy-done | bytes 131096
  1.8 0.8 %copy-done.3 = s32[128,128]{1,0:T(8,128)S(1)} copy-done((s32[128,128]{1,0:T(8,128)S(1)}, s32[128,128]{1,0:T(8,128)}, u32[]{:S(2)}) %copy-start.3) | copy-done | bytes 65560
  2.7 0.8 %copy-done.5 = s32[128,128]{1,0:T(8,128)S(1)} copy-done((s32[128,128]{1,0:T(8,128)S(1)}, s32[128,128]{1,0:T(8,128)}, u32[]{:S(2)}) %copy-start.5) | copy-done | bytes 65560
  3.5 0.8 %copy-done.7 = f32[128,128]{1,0:T(8,128)S(1)} copy-done((f32[128,128]{1,0:T(8,128)S(1)}, f32[128,128]{1,0:T(8,128)}, u32[]{:S(2)}) %copy-start.7) | copy-done | bytes 65560
  4.3 0.2 shard_map.55
  4.5 3.3 %collective-permute-start = (f32[16,128]{1,0:T(8,128)S(1)}, f32[16,128]{1,0:T(8,128)S(1)}, u32[]{:S(2)}, u32[]{:S(2)}) collective-permute-start(f32[16,128]{1,0:T(8,128)S(1)} %get-tuple-element.26), channel_id=1, source_target_pairs={{0,16},{16,0},{32,48},{48,32},{64,80},{80,64},{96,112},{112,96},{1... | collective-permute-start | bytes 24584 | tf_op jit(solution)/shard_map/ppermute | solution.py:463
  7.8 1.9 %collective-permute-start.1 = (f32[16,128]{1,0:T(8,128)S(1)}, f32[16,128]{1,0:T(8,128)S(1)}, u32[]{:S(2)}, u32[]{:S(2)}) collective-permute-start(f32[16,128]{1,0:T(8,128)S(1)} %get-tuple-element.27), channel_id=1, source_target_pairs={{16,32},{32,16},{48,64},{64,48},{80,96},{96,80},{112,128},{128,112... | collective-permute-start | bytes 24584 | tf_op jit(solution)/shard_map/ppermute | solution.py:463
  9.8 3.0 %collective-permute-done.1.got_b.cb = f32[16,128]{1,0:T(8,128)S(1)} collective-permute-done((f32[16,128]{1,0:T(8,128)S(1)}, f32[16,128]{1,0:T(8,128)S(1)}, u32[]{:S(2)}, u32[]{:S(2)}) %collective-permute-start.1) | collective-permute-done | bytes 8224 | tf_op jit(solution)/shard_map/ppermute | solution.py:463
  12.8 0.2 shard_map.56
  13.0 0.1 collective-permute-start.2
  13.1 0.7 collective-permute-start.3
  13.8 1.8 %collective-permute-done.2.ra = f32[16,128]{1,0:T(8,128)S(1)} collective-permute-done((f32[16,128]{1,0:T(8,128)S(1)}, f32[16,128]{1,0:T(8,128)S(1)}, u32[]{:S(2)}, u32[]{:S(2)}) %collective-permute-start.2) | collective-permute-done | bytes 8224 | tf_op jit(solution)/shard_map/ppermute | solution.py:463
  15.6 1.2 %shard_map.57 = (f32[256,128]{1,0:T(8,128)S(1)}, f32[128,128]{1,0:T(8,128)S(1)}, f32[128,128]{1,0:T(8,128)S(1)}, f32[128,128]{1,0:T(8,128)S(1)}, f32[5,2,128,128...) custom-call(f32[2,128,128]{2,1,0:T(8,128)S(1)} %copy-done.2, f32[2,128,128]{2,1,0:T(8,128)S(1)} %copy-done.1, ...), custom_call_target="tpu_custom_call" | custom-call | tf_op jit(solution)/shard_map/pallas_call | solution.py:450
  16.8 17.8 %all_to_all.20 = f32[16,16,128]{2,1,0:T(8,128)S(1)} all-to-all(f32[16,16,128]{2,1,0:T(8,128)S(1)} %bitcast.13), channel_id=1, replica_groups=mesh['gx'=16,'gy'=16] {'gx'}, dimensions={0} | all-to-all | bytes 262144 | tf_op jit(solution)/shard_map/all_to_all | solution.py:468
  34.6 0.7 shard_map.58
  35.3 0.0 copy-start.4
  35.3 0.0 copy-start.6
  35.3 19.1 %all_to_all.21 = f32[16,24,128]{2,1,0:T(8,128)S(1)} all-to-all(f32[16,24,128]{2,1,0:T(8,128)S(1)} %bitcast.12), channel_id=1, replica_groups=mesh['gx'=16,'gy'=16] {'gy'}, dimensions={0} | all-to-all | bytes 393216 | tf_op jit(solution)/shard_map/all_to_all | solution.py:468
  54.5 1.0 %shard_map.59 = (f32[128,128]{1,0:T(8,128)S(1)}, f32[128,128]{1,0:T(8,128)S(1)}, f32[128,128]{1,0:T(8,128)S(1)}, f32[128,128]{1,0:T(8,128)S(1)}, f32[5,1,128,128]{3,2,1,0:T(8,128)S(1)}) custom-call(f32[384,128]{1,0:T(8,128)S(1)} %bitcast.8, f32[3,2,128,128]{3,2,1,0:T(8,128)S(1)} %get-tuple-element.36.vp, f32[2,128,128]{2,1,0:T(8,128)S(1)} %get-tuple-element.37.u_new, ...), custom_call_target="tpu_custom_call" | custom-call | tf_op jit(solution)/shard_map/pallas_call | solution.py:450
  55.5 11.2 %all_to_all.22 = f32[16,8,128]{2,1,0:T(8,128)S(1)} all-to-all(f32[16,8,128]{2,1,0:T(8,128)S(1)} %bitcast.14), channel_id=1, replica_groups=mesh['gx'=16,'gy'=16] {'gx'}, dimensions={0} | all-to-all | bytes 131072 | tf_op jit(solution)/shard_map/all_to_all | solution.py:468
  66.8 0.4 shard_map.60
  67.2 9.2 %all_to_all.23 = f32[16,8,128]{2,1,0:T(8,128)S(1)} all-to-all(f32[16,8,128]{2,1,0:T(8,128)S(1)} %bitcast.15), channel_id=1, replica_groups=mesh['gx'=16,'gy'=16] {'gy'}, dimensions={0} | all-to-all | bytes 131072 | tf_op jit(solution)/shard_map/all_to_all | solution.py:468
  76.4 0.7 shard_map.61
  (11 shorter events, 0.0 us)
Async XLA Ops:
  0.0 0.9 %copy-start = (f32[2,128,128]{2,1,0:T(8,128)S(1)}, f32[2,128,128]{2,1,0:T(8,128)}, u32[]{:S(2)}) copy-start(f32[2,128,128]{2,1,0:T(8,128)} %wind.5) | copy-start | bytes 393220
  0.9 0.9 %copy-start.2 = (f32[2,128,128]{2,1,0:T(8,128)S(1)}, f32[2,128,128]{2,1,0:T(8,128)}, u32[]{:S(2)}) copy-start(f32[2,128,128]{2,1,0:T(8,128)} %vel.5) | copy-start | bytes 393220
  1.8 0.8 %copy-start.3 = (s32[128,128]{1,0:T(8,128)S(1)}, s32[128,128]{1,0:T(8,128)}, u32[]{:S(2)}) copy-start(s32[128,128]{1,0:T(8,128)} %ice.5) | copy-start | bytes 196612
  2.6 0.8 %copy-start.5 = (s32[128,128]{1,0:T(8,128)S(1)}, s32[128,128]{1,0:T(8,128)}, u32[]{:S(2)}) copy-start(s32[128,128]{1,0:T(8,128)} %land.5) | copy-start | bytes 196612
  3.5 0.8 %copy-start.7 = (f32[128,128]{1,0:T(8,128)S(1)}, f32[128,128]{1,0:T(8,128)}, u32[]{:S(2)}) copy-start(f32[128,128]{1,0:T(8,128)} %thick.5) | copy-start | bytes 196612
  4.5 11.1 %copy-start.1 = (f32[2,128,128]{2,1,0:T(8,128)S(1)}, f32[2,128,128]{2,1,0:T(8,128)}, u32[]{:S(2)}) copy-start(f32[2,128,128]{2,1,0:T(8,128)} %wind.5) | copy-start | bytes 393220
  4.5 5.2 %collective-permute-start = (f32[16,128]{1,0:T(8,128)S(1)}, f32[16,128]{1,0:T(8,128)S(1)}, u32[]{:S(2)}, u32[]{:S(2)}) collective-permute-start(f32[16,128]{1,0:T(8,128)S(1)} %get-tuple-element.26), channel_id=1, source_target_pairs={{0,16},{16,0},{32,48},{48,32},{64,80},{80,64},{96,112},{112,96},{1... | collective-permute-start | bytes 24584 | tf_op jit(solution)/shard_map/ppermute | solution.py:463
  7.8 5.0 %collective-permute-start.1 = (f32[16,128]{1,0:T(8,128)S(1)}, f32[16,128]{1,0:T(8,128)S(1)}, u32[]{:S(2)}, u32[]{:S(2)}) collective-permute-start(f32[16,128]{1,0:T(8,128)S(1)} %get-tuple-element.27), channel_id=1, source_target_pairs={{16,32},{32,16},{48,64},{64,48},{80,96},{96,80},{112,128},{128,112... | collective-permute-start | bytes 24584 | tf_op jit(solution)/shard_map/ppermute | solution.py:463
  13.0 2.6 %collective-permute-start.2 = (f32[16,128]{1,0:T(8,128)S(1)}, f32[16,128]{1,0:T(8,128)S(1)}, u32[]{:S(2)}, u32[]{:S(2)}) collective-permute-start(f32[16,128]{1,0:T(8,128)S(1)} %get-tuple-element.28), channel_id=1, source_target_pairs={{0,1},{1,0},{2,3},{3,2},{4,5},{5,4},{6,7},{7,6},{8,9},{9,8},{10,11... | collective-permute-start | bytes 24584 | tf_op jit(solution)/shard_map/ppermute | solution.py:463
  13.1 2.5 %collective-permute-start.3 = (f32[16,128]{1,0:T(8,128)S(1)}, f32[16,128]{1,0:T(8,128)S(1)}, u32[]{:S(2)}, u32[]{:S(2)}) collective-permute-start(f32[16,128]{1,0:T(8,128)S(1)} %get-tuple-element.29), channel_id=1, source_target_pairs={{1,2},{2,1},{3,4},{4,3},{5,6},{6,5},{7,8},{8,7},{9,10},{10,9},{11,... | collective-permute-start | bytes 24584 | tf_op jit(solution)/shard_map/ppermute | solution.py:463
  35.3 19.2 %copy-start.4 = (s32[128,128]{1,0:T(8,128)S(1)}, s32[128,128]{1,0:T(8,128)}, u32[]{:S(2)}) copy-start(s32[128,128]{1,0:T(8,128)} %ice.5) | copy-start | bytes 196612
  35.3 19.2 %copy-start.6 = (s32[128,128]{1,0:T(8,128)S(1)}, s32[128,128]{1,0:T(8,128)}, u32[]{:S(2)}) copy-start(s32[128,128]{1,0:T(8,128)} %land.5) | copy-start | bytes 196612

commit v2 on v1

--- a/solution.py
+++ b/solution.py
@@ -44,57 +44,97 @@
     return jnp.where(jnp.broadcast_to(flag, (rows, N)), a, b)
 
 
-def pack_columns(vel, wind, thick, ice, land, send_a, send_b, turn):
-    live = (ice[...] * (1 - land[...])).astype(F32)
+def edge_rows(vel, thick, send_a, send_b, low, high, sems):
+    copies = []
+    for k in range(3):
+        source = vel.at[k] if k < 2 else thick
+        copies.append(pltpu.make_async_copy(source.at[0:8], low.at[k], sems.at[2 * k]))
+        copies.append(pltpu.make_async_copy(source.at[N - 8 : N], high.at[k], sems.at[2 * k + 1]))
+    for c in copies:
+        c.start()
+    for c in copies:
+        c.wait()
+    even = lax.rem(lax.axis_index("gy"), 2) == 0
+    for k in range(3):
+        first, final = low[k, 0:2], high[k, 6:8]
+        send_a[2 * k : 2 * k + 2] = pick(even, 2, final, first)
+        send_b[2 * k : 2 * k + 2] = pick(even, 2, first, final)
+    send_a[6:8] = jnp.zeros((2, N), F32)
+    send_b[6:8] = jnp.zeros((2, N), F32)
+
+
+def load(vel, wind, thick, ice, land, vel_v, wind_v, thick_v, live_v, edges, ice_v, land_v, turn, sems):
+    pairs = ((vel, vel_v), (thick, thick_v), (ice, ice_v), (land, land_v), (wind, wind_v))
+    copies = [pltpu.make_async_copy(x, y, sems.at[k]) for k, (x, y) in enumerate(pairs)]
+    for c in copies:
+        c.start()
+    for c in copies:
+        c.wait()
+    live = (ice_v[...] * (1 - land_v[...])).astype(F32)
+    live_v[...] = live
     lane = lanes(N)
-    mixed = jnp.where(lane < 36, pltpu.roll(live, 32, 1), vel[0])
-    mixed = jnp.where(lane < 28, pltpu.roll(wind[1], 24, 1), mixed)
-    mixed = jnp.where(lane < 20, pltpu.roll(thick[...], 16, 1), mixed)
-    mixed = jnp.where(lane < 12, pltpu.roll(vel[1], 8, 1), mixed)
-    mixed = jnp.where(lane < 4, vel[0], mixed)
+    mixed = jnp.where(lane < 36, pltpu.roll(live, 32, 1), vel_v[0])
+    mixed = jnp.where(lane < 28, pltpu.roll(wind_v[1], 24, 1), mixed)
+    mixed = jnp.where(lane < 20, pltpu.roll(thick_v[...], 16, 1), mixed)
+    mixed = jnp.where(lane < 12, pltpu.roll(vel_v[1], 8, 1), mixed)
+    mixed = jnp.where(lane < 4, vel_v[0], mixed)
     turn[...] = mixed.T
-    left = [turn[0:4], turn[8:12], turn[16:20], turn[24:26], turn[32:34]]
-    right = [turn[124:128], turn[4:8], turn[12:16], turn[22:24], turn[30:32]]
+    left = ((0, 4), (8, 4), (16, 4), (24, 2), (32, 2))
+    right = ((124, 4), (4, 4), (12, 4), (22, 2), (30, 2))
+    for base, places in ((0, left), (16, right)):
+        for at, n in places:
+            edges[base : base + n] = turn[at : at + n]
+            base += n
+
+
+def both_ways(a, b, axis):
+    even = lax.rem(lax.axis_index(axis), 2) == 0
+    n = a.shape[0]
+    return pick(even, n, a, b), pick(even, n, b, a)
+
+
+def pack_columns(edges, ra, rb, send_a, send_b, turn):
+    turn[...] = jnp.zeros((N, N), F32)
+    for k in range(3):
+        above, below = both_ways(ra[2 * k : 2 * k + 2], rb[2 * k : 2 * k + 2], "gy")
+        turn[4 * k : 4 * k + 2] = below
+        turn[4 * k + 2 : 4 * k + 4] = above
+    turn[...] = turn[...].T
     even = lax.rem(lax.axis_index("gx"), 2) == 0
-    at = 0
-    for a, b in zip(left, right):
-        n = a.shape[0]
-        send_a[at : at + n] = pick(even, n, b, a)
-        send_b[at : at + n] = pick(even, n, a, b)
-        at += n
-
-
-def side_columns(got_a, got_b, turn):
-    even = lax.rem(lax.axis_index("gx"), 2) == 0
+    for at, n, left, right in (
+        (0, 16, edges[0:16], edges[16:32]),
+        (16, 4, turn[0:4], turn[N - 4 : N]),
+        (20, 4, jnp.zeros((4, N), F32), jnp.zeros((4, N), F32)),
+    ):
+        send_a[at : at + n] = pick(even, n, right, left)
+        send_b[at : at + n] = pick(even, n, left, right)
+
+
+def side_columns(ca, cb, turn):
     turn[...] = jnp.zeros((N, N), F32)
     places = ((0, 4, 0, 124), (4, 4, 8, 4), (8, 4, 16, 12), (12, 2, 24, 22), (14, 2, 32, 30))
     for at, n, low, high in places:
-        a, b = got_a[at : at + n], got_b[at : at + n]
-        turn[low : low + n] = pick(even, n, a, b)
-        turn[high : high + n] = pick(even, n, b, a)
-    return turn[...].T
+        after, before = both_ways(ca[at : at + n], cb[at : at + n], "gx")
+        turn[low : low + n] = after
+        turn[high : high + n] = before
+    mixed = turn[...].T
+    turn[...] = jnp.zeros((N, N), F32)
+    after, before = both_ways(ca[16:20], cb[16:20], "gx")
+    turn[0:4] = after
+    turn[N - 4 : N] = before
+    turn[...] = turn[...].T
+    return mixed
+
+
+def outer(x, fill=0.0):
+    lane = lanes(x.shape[0])
+    return jnp.where((lane < 2) | (lane >= N - 2), x, fill)
 
 
 def side_field(mixed, slot):
     lane = lanes(N)
     moved = mixed if slot == 0 else pltpu.roll(mixed, N - 8 * slot, 1)
     return jnp.where((lane < 4) | (lane >= 124), moved, 0.0)
-
-
-def pack_rows(vel, thick, got_a, got_b, send_a, send_b, turn, work):
-    mixed = side_columns(got_a, got_b, turn)
-    even = lax.rem(lax.axis_index("gy"), 2) == 0
-    for k in range(3):
-        turn[...] = side_field(mixed, k)
-        own = vel.at[k] if k < 2 else thick
-        for tile, source in ((0, own), (1, turn)):
-            low, high = source[0:2], source[126:128]
-            at = 8 * tile + 2 * k
-            send_a[at : at + 2] = pick(even, 2, high, low)
-            send_b[at : at + 2] = pick(even, 2, low, high)
-    for tile in (0, 1):
-        send_a[8 * tile + 6 : 8 * tile + 8] = jnp.zeros((2, N), F32)
-        send_b[8 * tile + 6 : 8 * tile + 8] = jnp.zeros((2, N), F32)
 
 
 def root_viscosity(su, sv, st, sh):
@@ -215,12 +255,11 @@
     return coupling, second, [lq, uq, rq]
 
 
-def solve_pieces(got, width, base, me, rowed, halo=None):
-    take = lambda k: got[pl.ds(base + k, K, width), :]
+def solve_pieces(take, me, rowed, extra=None):
     fl, fu, fe, fr, zl, zu, ze, zr = (take(k) for k in range(8))
     nxt = lambda a: pltpu.roll(a, K - 1, 0)
-    fe = nxt(fe)
-    uu, ee, rr = zu * nxt(fu), ze + zu * fe, zr + zu * nxt(fr)
+    fl, fu, fe, fr = nxt(fl), nxt(fu), nxt(fe), nxt(fr)
+    uu, ee, rr = zu * fu, ze + zu * fe, zr + zu * fr
     q = 1.0 / (zl + ee + uu)
     l, u, e, r = zl * q, uu * q, ee * q, rr * q
     s = 1
@@ -233,33 +272,44 @@
         q = 1.0 / (ll + uu + ee)
         l, u, e, r = ll * q, uu * q, ee * q, rr * q
         s *= 2
-    rowed[0:K] = jnp.zeros((K, N), F32)
+    zero = jnp.zeros((K, N), F32)
+    rowed[0:K] = zero
     rowed[K : 2 * K] = r
-    rowed[2 * K : 3 * K] = jnp.zeros((K, N), F32)
+    rowed[2 * K : 3 * K] = zero
     before, own = rowed[pl.ds(K - 1 + me, 1), :], rowed[pl.ds(K + me, 1), :]
-    if halo is None:
+    if extra is None:
         return before, own
     before2, after = rowed[pl.ds(K - 2 + me, 1), :], rowed[pl.ds(K + 1 + me, 1), :]
-    up = jnp.minimum(me + 1, K - 1) * width
-    down = jnp.maximum(me - 1, 0) * width
+    rowed[0:K] = jnp.where(sublanes(K) == K - 1, 0.0, fr + fl * r + fu * nxt(r))
+    first = rowed[pl.ds(me, 1), :]
+    up, down = extra
+    second = up(2) + up(0) * own + up(1) * after
+    ahead = down(2) + down(0) * before2 + down(1) * before
+    return before, own, ahead, first, second
+
+
+def rows_of(got, width):
+    return lambda k: got[pl.ds(k, K, width), :]
+
+
+def rows_beside(got, width, base, me):
+    up = jnp.minimum(me + 1, K - 1) * width + base
+    down = jnp.maximum(me - 1, 0) * width + base
     has_up = jnp.broadcast_to(me < K - 1, (1, N))
     has_down = jnp.broadcast_to(me > 0, (1, N))
-    row = lambda at, k: got[pl.ds(at + k, 1), :]
-    first = row(up, base + 3) + row(up, base) * own + row(up, base + 1) * after
-    first = jnp.where(has_up, first, 0.0)
-    second = row(up, halo + 2) + row(up, halo) * own + row(up, halo + 1) * after
-    second = jnp.where(has_up, second, 0.0)
-    ahead = row(down, halo + 2) + row(down, halo) * before2 + row(down, halo + 1) * before
-    ahead = jnp.where(has_down, ahead, 0.0)
-    return before, own, ahead, first, second
-
-
-def spread(dest, me, common, forward, backward, width):
+    return (
+        lambda k: jnp.where(has_up, got[pl.ds(up + k, 1), :], 0.0),
+        lambda k: jnp.where(has_down, got[pl.ds(down + k, 1), :], 0.0),
+    )
+
+
+def spread(dest, me, common, forward=None, backward=None):
+    width = 8 if forward is None else 16
     for d in range(K):
         at = d * width
-        dest[at : at + 8 * len(common)] = jnp.concatenate(common, 0) if len(common) > 1 else common[0]
+        dest[at : at + 8] = common
         if forward is not None:
-            dest[at + width - 8 : at + width] = pick(me < d, 8, forward, backward)
+            dest[at + 8 : at + 16] = pick(me < d, 8, forward, backward)
 
 
 def tile_of(rows, pad):
@@ -268,9 +318,8 @@
     return pad[...]
 
 
-def first_u(vel, wind, thick, ice, land, ca, cb, ra, rb, send, pl_, pu_, pr_, vsys, sth, su, sv, st, sh, turn, tall, bands, pad):
+def first_u(vel, wind, thick, alive, ra, rb, ca, cb, send, pl_, pu_, pr_, vsys, sth, su, sv, st, sh, turn, tall, bands, pad):
     mixed = side_columns(ca, cb, turn)
-    even = lax.rem(lax.axis_index("gy"), 2) == 0
     zero = jnp.zeros((TOP, N), F32)
     for k, s in enumerate((su, sv, st)):
         own = vel.at[k] if k < 2 else thick
@@ -278,18 +327,17 @@
             s[t, 0:TOP] = zero
             s[t, TOP + N :] = zero
             s[t, TOP : TOP + N] = own[...] if t == 0 else side_field(mixed, k)
-            at = 8 * t + 2 * k
-            a, b = ra[at : at + 2], rb[at : at + 2]
-            s[t, TOP + N : TOP + N + 2] = pick(even, 2, a, b)
-            s[t, TOP - 2 : TOP] = pick(even, 2, b, a)
+        above, below = both_ways(ra[2 * k : 2 * k + 2], rb[2 * k : 2 * k + 2], "gy")
+        s[0, TOP - 2 : TOP] = below
+        s[0, TOP + N : TOP + N + 2] = above
+        s[1, TOP - 2 : TOP] = turn[4 * k : 4 * k + 2]
+        s[1, TOP + N : TOP + N + 2] = turn[4 * k + 2 : 4 * k + 4]
     tall[0] = side_field(mixed, 3)
     tall[1] = side_field(mixed, 4)
     root_viscosity(su, sv, st, sh)
 
     def live(t, cell):
-        if t == 0:
-            return (ice[cell] * (1 - land[cell])).astype(F32)
-        return tall[1, cell]
+        return alive[cell] if t == 0 else tall[1, cell]
 
     def wy(t, cell):
         return wind[1, cell] if t == 0 else tall[0, cell]
@@ -323,7 +371,7 @@
     pad[...] = jnp.zeros((8, N), F32)
     forward = tile_of(ahead, pad)
     backward = tile_of(second, pad)
-    spread(send, me, [common], forward, backward, 16)
+    spread(send, me, common, forward, backward)
 
 
 def load_v(bands, vsys, t, speed):
@@ -340,7 +388,7 @@
 
 def first_v(got, pl_, pu_, pr_, vsys, send, u_new, vp, turn, bands, pad, rowed):
     me = lax.axis_index("gx")
-    before, own, ahead, first, second = solve_pieces(got, 16, 0, me, rowed, 8)
+    before, own, ahead, first, second = solve_pieces(rows_of(got, 16), me, rowed, rows_beside(got, 16, 8, me))
     turn[...] = pr_[...] + pl_[...] * before + pu_[...] * own
     u_new[0] = turn[...].T
     turn[...] = jnp.zeros((N, N), F32)
@@ -349,7 +397,6 @@
     turn[N - 2 : N - 1] = ahead
     turn[N - 1 : N] = before
     u_new[1] = turn[...].T
-    mains = []
     for t in (0, 1):
         last = load_v(bands, vsys, t, u_new[t])
 
@@ -358,26 +405,29 @@
                 vp[min(k, 2), t, at : at + 8] = x
 
         main, second, ahead = reduce_piece(bands, last, out)
-        mains.append(tile_of(main, pad))
         if t == 0:
-            extras = (ahead, second)
+            common, extras = tile_of(main, pad), (ahead, second)
+    packed = jnp.zeros((1, N), F32)
+    inward = lambda x, at: pltpu.roll(jnp.where(lanes(1) < 4, pltpu.roll(x, 2, 1), 0.0), at, 1)
+    for k, x in enumerate(main):
+        packed = packed + (inward(x, 4 * k) if k else jnp.where(lanes(1) < 4, pltpu.roll(x, 2, 1), 0.0))
     pad[...] = jnp.zeros((8, N), F32)
-    last_rows = [u_new[0, N - 2 : N - 1], u_new[0, N - 1 : N], u_new[1, N - 1 : N]]
-    first_rows = [u_new[0, 1:2], u_new[0, 0:1], u_new[1, 0:1]]
-    forward = tile_of(extras[0] + last_rows, pad)
-    backward = tile_of(extras[1] + first_rows, pad)
-    spread(send, lax.axis_index("gy"), mains, forward, backward, 24)
-
-
-def second_u(got, vp, u_new, sth, wind, ice, land, send, pl_, pu_, pr_, vsys, su, sv, sh, tall, bands, pad, rowed):
+    forward = tile_of(
+        [packed + inward(u_new[1, N - 1 : N], 32)] + extras[0] + [u_new[0, N - 2 : N - 1], u_new[0, N - 1 : N]], pad
+    )
+    backward = tile_of([packed + inward(u_new[1, 0:1], 32)] + extras[1] + [u_new[0, 1:2], u_new[0, 0:1]], pad)
+    spread(send, lax.axis_index("gy"), common, forward, backward)
+
+
+def second_u(got, vp, u_new, sth, wind, alive, send, pl_, pu_, pr_, vsys, su, sv, sh, tall, bands, pad, rowed):
     me = lax.axis_index("gy")
-    up = jnp.minimum(me + 1, K - 1) * 24
-    down = jnp.maximum(me - 1, 0) * 24
-    has_up = jnp.broadcast_to(me < K - 1, (1, N))
-    has_down = jnp.broadcast_to(me > 0, (1, N))
+    up, down = rows_beside(got, 16, 8, me)
+    coefs = (lambda k: up(1 + k), lambda k: down(1 + k))
+    packed = got[pl.ds(8, K, 16), :]
+    unpack = lambda k: outer(pltpu.roll(packed, N - 2 - 4 * k, 1), 1.0 if k in (2, 6) else 0.0)
     zero = jnp.zeros((TOP, N), F32)
     for t in (0, 1):
-        before, own, ahead, first, second = solve_pieces(got, 24, 8 * t, me, rowed, 16)
+        before, own, ahead, first, second = solve_pieces(rows_of(got, 16) if t == 0 else unpack, me, rowed, coefs)
         for s in (su, sv):
             s[t, 0:TOP] = zero
             s[t, TOP + N :] = zero
@@ -385,19 +435,20 @@
         sv[t, TOP - 1 : TOP] = before
         sv[t, TOP + N : TOP + N + 1] = first
         su[t, TOP : TOP + N] = u_new[t]
-        near = 20 if t == 0 else 21
-        row = lambda at, k: got[pl.ds(at + k, 1), :]
-        su[t, TOP - 1 : TOP] = jnp.where(has_down, row(down, near), 0.0)
-        su[t, TOP + N : TOP + N + 1] = jnp.where(has_up, row(up, near), 0.0)
         if t == 0:
             sv[0, TOP - 2 : TOP - 1] = ahead
             sv[0, TOP + N + 1 : TOP + N + 2] = second
-            su[0, TOP - 2 : TOP - 1] = jnp.where(has_down, row(down, 19), 0.0)
-            su[0, TOP + N + 1 : TOP + N + 2] = jnp.where(has_up, row(up, 19), 0.0)
+            su[0, TOP - 2 : TOP - 1] = down(4)
+            su[0, TOP - 1 : TOP] = down(5)
+            su[0, TOP + N : TOP + N + 1] = up(5)
+            su[0, TOP + N + 1 : TOP + N + 2] = up(4)
+        else:
+            su[1, TOP - 1 : TOP] = outer(pltpu.roll(down(0), N - 34, 1))
+            su[1, TOP + N : TOP + N + 1] = outer(pltpu.roll(up(0), N - 34, 1))
     root_viscosity(su, sv, sth, sh)
 
     def live(t, cell):
-        return (ice[cell] * (1 - land[cell])).astype(F32)
+        return alive[cell]
 
     def put_u(cell, *values):
         for k, x in enumerate(values):
@@ -421,11 +472,11 @@
             outs[k][at : at + 8] = x
 
     main, _, _ = reduce_piece(bands, last, out)
-    spread(send, lax.axis_index("gx"), [tile_of(main, pad)], None, None, 8)
+    spread(send, lax.axis_index("gx"), tile_of(main, pad))
 
 
 def second_v(got, pl_, pu_, pr_, vsys, send, u_new, vp, turn, bands, pad, rowed):
-    before, own = solve_pieces(got, 8, 0, lax.axis_index("gx"), rowed)
+    before, own = solve_pieces(rows_of(got, 8), lax.axis_index("gx"), rowed)
     turn[...] = pr_[...] + pl_[...] * before + pu_[...] * own
     u_new[...] = turn[...].T
     last = load_v(bands, vsys, 0, u_new[...])
@@ -435,25 +486,27 @@
             vp[min(k, 2), at : at + 8] = x
 
     main, _, _ = reduce_piece(bands, last, out)
-    spread(send, lax.axis_index("gy"), [tile_of(main, pad)], None, None, 8)
+    spread(send, lax.axis_index("gy"), tile_of(main, pad))
 
 
 def finish(got, vp, u_new, out, rowed):
-    before, own = solve_pieces(got, 8, 0, lax.axis_index("gy"), rowed)
+    before, own = solve_pieces(rows_of(got, 8), lax.axis_index("gy"), rowed)
     out[0] = u_new[...]
     out[1] = vp[2] + vp[0] * before + vp[1] * own
 
 
-def call(kernel, outs, scratch, *args):
+def call(kernel, outs, scratch, *args, far=False, flops=None):
     vmem = pl.BlockSpec(memory_space=pltpu.VMEM)
     shapes = [jax.ShapeDtypeStruct(s, F32) for s in outs]
+    cost = None if flops is None else pl.CostEstimate(flops=flops, bytes_accessed=0, transcendentals=0)
     return pl.pallas_call(
         kernel,
         out_shape=shapes,
-        in_specs=[vmem] * len(args),
+        in_specs=[pl.BlockSpec(memory_space=pltpu.HBM) if far else vmem] * len(args),
         out_specs=[vmem] * len(outs),
-        scratch_shapes=[pltpu.VMEM(s, F32) for s in scratch],
+        scratch_shapes=[pltpu.VMEM(s, F32) if isinstance(s, tuple) else s for s in scratch],
         compiler_params=pltpu.CompilerParams(vmem_limit_bytes=8 * 1024 * 1024),
+        cost_estimate=cost,
     )(*args)
 
 
@@ -472,20 +525,29 @@
 def on_device(velocity, wind, thick, ice, land):
     square, halves, rim = (N, N), (2, N, N), (2, ROWS, N)
     bands, pad, rowed = (2, 4, N + 16, N), (8, N), (3 * K, N)
-    a, b = call(pack_columns, [(16, N)] * 2, [square], velocity, wind, thick, ice, land)
+    flags = pltpu.VMEM(square, jnp.int32)
+    sems = pltpu.SemaphoreType.DMA((6,))
+    a, b = call(edge_rows, [(8, N)] * 2, [(3, 8, N)] * 2 + [sems], velocity, thick, far=True)
+    ra, rb = neighbours(a, b, "gy")
+    vel, wind, thick, alive, edges = call(
+        load,
+        [halves, halves, square, square, (32, N)],
+        [flags, flags, square, sems],
+        velocity, wind, thick, ice, land,
+        far=True, flops=10**8,
+    )
+    a, b = call(pack_columns, [(24, N)] * 2, [square], edges, ra, rb)
     ca, cb = neighbours(a, b, "gx")
-    a, b = call(pack_rows, [(16, N)] * 2, [square, pad], velocity, thick, ca, cb)
-    ra, rb = neighbours(a, b, "gy")
     send, l, u, r, vsys, sth = call(
         first_u,
         [(K * 16, N), square, square, square, (5,) + halves, rim],
         [rim] * 4 + [square, (6, N, N), bands, pad],
-        velocity, wind, thick, ice, land, ca, cb, ra, rb,
+        vel, wind, thick, alive, ra, rb, ca, cb,
     )
     got = share(send, "gx")
     send, u_new, vp = call(
         first_v,
-        [(K * 24, N), halves, (3,) + halves],
+        [(K * 16, N), halves, (3,) + halves],
         [square, bands, pad, rowed],
         got, l, u, r, vsys,
     )
@@ -494,7 +556,7 @@
         second_u,
         [(K * 8, N), square, square, square, (5, 1, N, N)],
         [rim] * 3 + [(4, N, N), bands, pad, rowed],
-        got, vp, u_new, sth, wind, ice, land,
+        got, vp, u_new, sth, wind, alive,
     )
     got = share(send, "gx")
     send, u_new, vp = call(

time: 77.6 us -> 74.2 us (0.956)
  waiting for transfers between devices: 4.85 us -> 2.15 us
  blocking collectives: 57.5 us -> 55.8 us
  starting transfers between devices: 5.95 us -> 7.25 us
  local copies, waits for them, and re-layouts: 4.34 us -> 3.42 us
    ppermute x4, waiting for transfers between devices: 4.85 us -> 2.15 us  [neighbours(): return (lax.ppermute(a, axis, inner), lax.ppermute(b, axis, outer))]
    all_to_all x4, blocking collectives: 57.5 us -> 55.8 us  [share(): moved = lax.all_to_all(rows.reshape(K, width, N), axis, 0, 0, tiled=True)]
    ppermute x4, starting transfers between devices: 5.95 us -> 7.25 us  [neighbours(): return (lax.ppermute(a, axis, inner), lax.ppermute(b, axis, outer))]
    unnamed x16 -> x12, local copies, waits for them, and re-layouts: 4.34 us -> 3.42 us
    pallas_call x7 -> x8, Pallas kernels: 4.45 us -> 5.07 us  [call(): pl.pallas_call(kernel, out_shape=shapes, in_specs=[pl.BlockSpec(memory_sp...]
  transfers between devices with their start and end apart: 4 -> 4, of which waited for: 2 -> 1; matrix products, arithmetic and copies ran while one was open for 0% -> 0% of each run, Pallas kernels for 0% -> 1%
where the time goes in v2:
time: 74.2 us; the launch traced here: 73.8 us
  blocking collectives  55.8 us (75%)
  starting transfers between devices  7.25 us (10%)
  Pallas kernels  5.07 us (7%)
  local copies, waits for them, and re-layouts  3.42 us (5%)
  waiting for transfers between devices  2.15 us (3%)
    all_to_all x4, blocking collectives, share(): moved = lax.all_to_all(rows.reshape(K, width, N), axis, 0, 0, tiled=True)  55.8 us
    ppermute x4, starting transfers between devices, neighbours(): return (lax.ppermute(a, axis, inner), lax.ppermute(b, axis, outer))  7.25 us
    pallas_call x8, Pallas kernels, call(): pl.pallas_call(kernel, out_shape=shapes, in_specs=[pl.BlockSpec(memory_sp...  5.07 us
    unnamed x12, local copies, waits for them, and re-layouts  3.42 us
    ppermute x4, waiting for transfers between devices, neighbours(): return (lax.ppermute(a, axis, inner), lax.ppermute(b, axis, outer))  2.15 us
  transfers between devices with their start and end apart: 4, of which 1 were waited for; matrix products, arithmetic and copies ran while one was open for 0% of the time, Pallas kernels for 1%

profile of v2, /device:TPU:1, one launch (start us, length us, event | category | flops | bytes accessed | tf_op | source)
XLA Modules:
  0.0 73.8 jit_solution(7672709421776782147)
XLA Ops:
  0.0 0.9 %copy-done = f32[2,128,128]{2,1,0:T(8,128)S(1)} copy-done((f32[2,128,128]{2,1,0:T(8,128)S(1)}, f32[2,128,128]{2,1,0:T(8,128)}, u32[]{:S(2)}) %copy-start) | copy-done | bytes 131096
  0.9 0.8 %copy-done.1 = f32[128,128]{1,0:T(8,128)S(1)} copy-done((f32[128,128]{1,0:T(8,128)S(1)}, f32[128,128]{1,0:T(8,128)}, u32[]{:S(2)}) %copy-start.1) | copy-done | bytes 65560
  1.7 0.1 shard_map.56
  1.9 2.1 %collective-permute-start = (f32[8,128]{1,0:T(8,128)S(1)}, f32[8,128]{1,0:T(8,128)S(1)}, u32[]{:S(2)}, u32[]{:S(2)}) collective-permute-start(f32[8,128]{1,0:T(8,128)S(1)} %get-tuple-element.35), channel_id=1, source_target_pairs={{0,1},{1,0},{2,3},{3,2},{4,5},{5,4},{6,7},{7,6},{8,9},{9,8},{10,11... | collective-permute-start | bytes 12296 | tf_op jit(solution)/shard_map/ppermute | solution.py:516
  4.0 0.6 collective-permute-start.1
  4.6 0.0 copy-start.4
  4.7 0.8 %copy-done.4 = s32[128,128]{1,0:T(8,128)S(1)} copy-done((s32[128,128]{1,0:T(8,128)S(1)}, s32[128,128]{1,0:T(8,128)}, u32[]{:S(2)}) %copy-start.4) | copy-done | bytes 65560
  5.5 0.8 %copy-done.5 = s32[128,128]{1,0:T(8,128)S(1)} copy-done((s32[128,128]{1,0:T(8,128)S(1)}, s32[128,128]{1,0:T(8,128)}, u32[]{:S(2)}) %copy-start.5) | copy-done | bytes 65560
  6.3 0.8 %shard_map.55 = (f32[2,128,128]{2,1,0:T(8,128)S(1)}, f32[2,128,128]{2,1,0:T(8,128)S(1)}, f32[128,128]{1,0:T(8,128)S(1)}, f32[128,128]{1,0:T(8,128)S(1)}, f32[32,128]{1,0:T(8,128)S(1)}) custom-call(f32[2,128,128]{2,1,0:T(8,128)S(1)} %copy-done, f32[2,128,128]{2,1,0:T(8,128)S(1)} %copy-done.3, f32[128,128]{1,0:T(8,128)S(1)} %copy-done.2, ...), custom_call_target="tpu_custom_call" | custom-call | flops 100000000 | tf_op jit(solution)/shard_map/pallas_call | solution.py:502
  7.2 0.0 collective-permute-done.ra
  7.2 0.0 collective-permute-done.1.rb
  7.2 0.1 shard_map.57
  7.3 1.6 %collective-permute-start.2 = (f32[24,128]{1,0:T(8,128)S(1)}, f32[24,128]{1,0:T(8,128)S(1)}, u32[]{:S(2)}, u32[]{:S(2)}) collective-permute-start(f32[24,128]{1,0:T(8,128)S(1)} %get-tuple-element.38), channel_id=1, source_target_pairs={{0,16},{16,0},{32,48},{48,32},{64,80},{80,64},{96,112},{112,96},{1... | collective-permute-start | bytes 36872 | tf_op jit(solution)/shard_map/ppermute | solution.py:516
  8.9 2.8 %collective-permute-start.3 = (f32[24,128]{1,0:T(8,128)S(1)}, f32[24,128]{1,0:T(8,128)S(1)}, u32[]{:S(2)}, u32[]{:S(2)}) collective-permute-start(f32[24,128]{1,0:T(8,128)S(1)} %get-tuple-element.39), channel_id=1, source_target_pairs={{16,32},{32,16},{48,64},{64,48},{80,96},{96,80},{112,128},{128,112... | collective-permute-start | bytes 36872 | tf_op jit(solution)/shard_map/ppermute | solution.py:516
  11.8 2.1 %collective-permute-done.3.cb = f32[24,128]{1,0:T(8,128)S(1)} collective-permute-done((f32[24,128]{1,0:T(8,128)S(1)}, f32[24,128]{1,0:T(8,128)S(1)}, u32[]{:S(2)}, u32[]{:S(2)}) %collective-permute-start.3) | collective-permute-done | bytes 12320 | tf_op jit(solution)/shard_map/ppermute | solution.py:516
  13.9 1.2 %shard_map.58 = (f32[256,128]{1,0:T(8,128)S(1)}, f32[128,128]{1,0:T(8,128)S(1)}, f32[128,128]{1,0:T(8,128)S(1)}, f32[128,128]{1,0:T(8,128)S(1)}, f32[5,2,128,128...) custom-call(f32[2,128,128]{2,1,0:T(8,128)S(1)} %get-tuple-element.31.vel, f32[2,128,128]{2,1,0:T(8,128)S(1)} %get-tuple-element.32.wind, ...), custom_call_target="tpu_custom_call" | custom-call | tf_op jit(solution)/shard_map/pallas_call | solution.py:502
  15.1 17.8 %all_to_all.20 = f32[16,16,128]{2,1,0:T(8,128)S(1)} all-to-all(f32[16,16,128]{2,1,0:T(8,128)S(1)} %bitcast.12), channel_id=1, replica_groups=mesh['gx'=16,'gy'=16] {'gx'}, dimensions={0} | all-to-all | bytes 262144 | tf_op jit(solution)/shard_map/all_to_all | solution.py:521
  32.9 0.7 %shard_map.59 = (f32[256,128]{1,0:T(8,128)S(1)}, f32[2,128,128]{2,1,0:T(8,128)S(1)}, f32[3,2,128,128]{3,2,1,0:T(8,128)S(1)}) custom-call(f32[256,128]{1,0:T(8,128)S(1)} %bitcast.8, f32[128,128]{1,0:T(8,128)S(1)} %get-tuple-element.41.pl_, f32[128,128]{1,0:T(8,128)S(1)} %get-tuple-element.42.pu_, f32[128,128]{1,0:T(8,128)S(1)} %get-tuple-element.43.pr_, ...), custom_call_target="tpu_custom_call" | custom-call | tf_op jit(solution)/shard_map/pallas_call | solution.py:502
  33.6 17.2 %all_to_all.21 = f32[16,16,128]{2,1,0:T(8,128)S(1)} all-to-all(f32[16,16,128]{2,1,0:T(8,128)S(1)} %bitcast.13), channel_id=1, replica_groups=mesh['gx'=16,'gy'=16] {'gy'}, dimensions={0} | all-to-all | bytes 262144 | tf_op jit(solution)/shard_map/all_to_all | solution.py:521
  50.9 1.0 %shard_map.60 = (f32[128,128]{1,0:T(8,128)S(1)}, f32[128,128]{1,0:T(8,128)S(1)}, f32[128,128]{1,0:T(8,128)S(1)}, f32[128,128]{1,0:T(8,128)S(1)}, f32[5,1,128,128]{3,2,1,0:T(8,128)S(1)}) custom-call(f32[256,128]{1,0:T(8,128)S(1)} %bitcast.9, f32[3,2,128,128]{3,2,1,0:T(8,128)S(1)} %get-tuple-element.46.vp, f32[2,128,128]{2,1,0:T(8,128)S(1)} %get-tuple-element.47.u_new, ...), custom_call_target="tpu_custom_call" | custom-call | tf_op jit(solution)/shard_map/pallas_call | solution.py:502
  51.9 11.5 %all_to_all.22 = f32[16,8,128]{2,1,0:T(8,128)S(1)} all-to-all(f32[16,8,128]{2,1,0:T(8,128)S(1)} %bitcast.14), channel_id=1, replica_groups=mesh['gx'=16,'gy'=16] {'gx'}, dimensions={0} | all-to-all | bytes 131072 | tf_op jit(solution)/shard_map/all_to_all | solution.py:521
  63.3 0.4 shard_map.61
  63.7 9.3 %all_to_all.23 = f32[16,8,128]{2,1,0:T(8,128)S(1)} all-to-all(f32[16,8,128]{2,1,0:T(8,128)S(1)} %bitcast.15), channel_id=1, replica_groups=mesh['gx'=16,'gy'=16] {'gy'}, dimensions={0} | all-to-all | bytes 131072 | tf_op jit(solution)/shard_map/all_to_all | solution.py:521
  73.1 0.7 %shard_map.62 = f32[2,128,128]{2,1,0:T(8,128)} custom-call(f32[128,128]{1,0:T(8,128)S(1)} %bitcast.11, f32[3,128,128]{2,1,0:T(8,128)S(1)} %get-tuple-element.55.vp, f32[128,128]{1,0:T(8,128)S(1)} %get-tuple-element.56.u_new), custom_call_target="tpu_custom_call" | custom-call | tf_op jit(solution)/shard_map/pallas_call | solution.py:502
  (8 shorter events, 0.0 us)
Async XLA Ops:
  0.0 0.9 %copy-start = (f32[2,128,128]{2,1,0:T(8,128)S(1)}, f32[2,128,128]{2,1,0:T(8,128)}, u32[]{:S(2)}) copy-start(f32[2,128,128]{2,1,0:T(8,128)} %vel.3) | copy-start | bytes 393220
  0.9 0.8 %copy-start.1 = (f32[128,128]{1,0:T(8,128)S(1)}, f32[128,128]{1,0:T(8,128)}, u32[]{:S(2)}) copy-start(f32[128,128]{1,0:T(8,128)} %thick.3) | copy-start | bytes 196612
  1.7 2.9 %copy-start.2 = (f32[128,128]{1,0:T(8,128)S(1)}, f32[128,128]{1,0:T(8,128)}, u32[]{:S(2)}) copy-start(f32[128,128]{1,0:T(8,128)} %thick.3) | copy-start | bytes 196612
  1.7 2.9 %copy-start.3 = (f32[2,128,128]{2,1,0:T(8,128)S(1)}, f32[2,128,128]{2,1,0:T(8,128)}, u32[]{:S(2)}) copy-start(f32[2,128,128]{2,1,0:T(8,128)} %wind.1) | copy-start | bytes 393220
  1.9 5.3 %collective-permute-start = (f32[8,128]{1,0:T(8,128)S(1)}, f32[8,128]{1,0:T(8,128)S(1)}, u32[]{:S(2)}, u32[]{:S(2)}) collective-permute-start(f32[8,128]{1,0:T(8,128)S(1)} %get-tuple-element.35), channel_id=1, source_target_pairs={{0,1},{1,0},{2,3},{3,2},{4,5},{5,4},{6,7},{7,6},{8,9},{9,8},{10,11... | collective-permute-start | bytes 12296 | tf_op jit(solution)/shard_map/ppermute | solution.py:516
  4.0 3.2 %collective-permute-start.1 = (f32[8,128]{1,0:T(8,128)S(1)}, f32[8,128]{1,0:T(8,128)S(1)}, u32[]{:S(2)}, u32[]{:S(2)}) collective-permute-start(f32[8,128]{1,0:T(8,128)S(1)} %get-tuple-element.36), channel_id=1, source_target_pairs={{1,2},{2,1},{3,4},{4,3},{5,6},{6,5},{7,8},{8,7},{9,10},{10,9},{11,... | collective-permute-start | bytes 12296 | tf_op jit(solution)/shard_map/ppermute | solution.py:516
  4.6 0.8 %copy-start.4 = (s32[128,128]{1,0:T(8,128)S(1)}, s32[128,128]{1,0:T(8,128)}, u32[]{:S(2)}) copy-start(s32[128,128]{1,0:T(8,128)} %ice.1) | copy-start | bytes 196612
  5.5 0.8 %copy-start.5 = (s32[128,128]{1,0:T(8,128)S(1)}, s32[128,128]{1,0:T(8,128)}, u32[]{:S(2)}) copy-start(s32[128,128]{1,0:T(8,128)} %land.1) | copy-start | bytes 196612
  7.3 4.5 %collective-permute-start.2 = (f32[24,128]{1,0:T(8,128)S(1)}, f32[24,128]{1,0:T(8,128)S(1)}, u32[]{:S(2)}, u32[]{:S(2)}) collective-permute-start(f32[24,128]{1,0:T(8,128)S(1)} %get-tuple-element.38), channel_id=1, source_target_pairs={{0,16},{16,0},{32,48},{48,32},{64,80},{80,64},{96,112},{112,96},{1... | collective-permute-start | bytes 36872 | tf_op jit(solution)/shard_map/ppermute | solution.py:516
  8.9 5.0 %collective-permute-start.3 = (f32[24,128]{1,0:T(8,128)S(1)}, f32[24,128]{1,0:T(8,128)S(1)}, u32[]{:S(2)}, u32[]{:S(2)}) collective-permute-start(f32[24,128]{1,0:T(8,128)S(1)} %get-tuple-element.39), channel_id=1, source_target_pairs={{16,32},{32,16},{48,64},{64,48},{80,96},{96,80},{112,128},{128,112... | collective-permute-start | bytes 36872 | tf_op jit(solution)/shard_map/ppermute | solution.py:516

commit v3 on v2

--- a/solution.py
+++ b/solution.py
@@ -4,6 +4,7 @@
 from jax.experimental import pallas as pl
 from jax.experimental.pallas import tpu as pltpu
 from jax.sharding import PartitionSpec as P
+
 
 CORIOLIS = 1.0
 DELTA_MIN = 0.25
@@ -44,40 +45,24 @@
     return jnp.where(jnp.broadcast_to(flag, (rows, N)), a, b)
 
 
-def edge_rows(vel, thick, send_a, send_b, low, high, sems):
-    copies = []
-    for k in range(3):
-        source = vel.at[k] if k < 2 else thick
-        copies.append(pltpu.make_async_copy(source.at[0:8], low.at[k], sems.at[2 * k]))
-        copies.append(pltpu.make_async_copy(source.at[N - 8 : N], high.at[k], sems.at[2 * k + 1]))
-    for c in copies:
-        c.start()
-    for c in copies:
-        c.wait()
+def edge_rows(vel, thick_low, thick_high, send_a, send_b):
     even = lax.rem(lax.axis_index("gy"), 2) == 0
     for k in range(3):
-        first, final = low[k, 0:2], high[k, 6:8]
+        first = vel[k, 0:2] if k < 2 else thick_low[...]
+        final = vel[k, N - 2 : N] if k < 2 else thick_high[...]
         send_a[2 * k : 2 * k + 2] = pick(even, 2, final, first)
         send_b[2 * k : 2 * k + 2] = pick(even, 2, first, final)
     send_a[6:8] = jnp.zeros((2, N), F32)
     send_b[6:8] = jnp.zeros((2, N), F32)
 
 
-def load(vel, wind, thick, ice, land, vel_v, wind_v, thick_v, live_v, edges, ice_v, land_v, turn, sems):
-    pairs = ((vel, vel_v), (thick, thick_v), (ice, ice_v), (land, land_v), (wind, wind_v))
-    copies = [pltpu.make_async_copy(x, y, sems.at[k]) for k, (x, y) in enumerate(pairs)]
-    for c in copies:
-        c.start()
-    for c in copies:
-        c.wait()
-    live = (ice_v[...] * (1 - land_v[...])).astype(F32)
-    live_v[...] = live
+def edge_columns(vel, wind, thick, alive, edges, turn):
     lane = lanes(N)
-    mixed = jnp.where(lane < 36, pltpu.roll(live, 32, 1), vel_v[0])
-    mixed = jnp.where(lane < 28, pltpu.roll(wind_v[1], 24, 1), mixed)
-    mixed = jnp.where(lane < 20, pltpu.roll(thick_v[...], 16, 1), mixed)
-    mixed = jnp.where(lane < 12, pltpu.roll(vel_v[1], 8, 1), mixed)
-    mixed = jnp.where(lane < 4, vel_v[0], mixed)
+    mixed = jnp.where(lane < 36, pltpu.roll(alive[...], 32, 1), vel[0])
+    mixed = jnp.where(lane < 28, pltpu.roll(wind[1], 24, 1), mixed)
+    mixed = jnp.where(lane < 20, pltpu.roll(thick[...], 16, 1), mixed)
+    mixed = jnp.where(lane < 12, pltpu.roll(vel[1], 8, 1), mixed)
+    mixed = jnp.where(lane < 4, vel[0], mixed)
     turn[...] = mixed.T
     left = ((0, 4), (8, 4), (16, 4), (24, 2), (32, 2))
     right = ((124, 4), (4, 4), (12, 4), (22, 2), (30, 2))
@@ -495,16 +480,16 @@
     out[1] = vp[2] + vp[0] * before + vp[1] * own
 
 
-def call(kernel, outs, scratch, *args, far=False, flops=None):
+def call(kernel, outs, scratch, *args, flops=None):
     vmem = pl.BlockSpec(memory_space=pltpu.VMEM)
     shapes = [jax.ShapeDtypeStruct(s, F32) for s in outs]
     cost = None if flops is None else pl.CostEstimate(flops=flops, bytes_accessed=0, transcendentals=0)
     return pl.pallas_call(
         kernel,
         out_shape=shapes,
-        in_specs=[pl.BlockSpec(memory_space=pltpu.HBM) if far else vmem] * len(args),
+        in_specs=[vmem] * len(args),
         out_specs=[vmem] * len(outs),
-        scratch_shapes=[pltpu.VMEM(s, F32) if isinstance(s, tuple) else s for s in scratch],
+        scratch_shapes=[pltpu.VMEM(s, F32) for s in scratch],
         compiler_params=pltpu.CompilerParams(vmem_limit_bytes=8 * 1024 * 1024),
         cost_estimate=cost,
     )(*args)
@@ -513,7 +498,9 @@
 def neighbours(a, b, axis):
     inner = [(i, i ^ 1) for i in range(K)]
     outer = [p for i in range(1, K - 1, 2) for p in ((i, i + 1), (i + 1, i))]
-    return lax.ppermute(a, axis, inner), lax.ppermute(b, axis, outer)
+    far = lax.ppermute(b, axis, outer)
+    near = lax.ppermute(a, axis, inner)
+    return near, far
 
 
 def share(rows, axis):
@@ -522,20 +509,13 @@
     return moved.reshape(K * width, N)
 
 
-def on_device(velocity, wind, thick, ice, land):
+def on_device(vel, wind, thick, ice, land):
     square, halves, rim = (N, N), (2, N, N), (2, ROWS, N)
     bands, pad, rowed = (2, 4, N + 16, N), (8, N), (3 * K, N)
-    flags = pltpu.VMEM(square, jnp.int32)
-    sems = pltpu.SemaphoreType.DMA((6,))
-    a, b = call(edge_rows, [(8, N)] * 2, [(3, 8, N)] * 2 + [sems], velocity, thick, far=True)
+    a, b = call(edge_rows, [(8, N)] * 2, [], vel, thick[:2], thick[N - 2 :])
     ra, rb = neighbours(a, b, "gy")
-    vel, wind, thick, alive, edges = call(
-        load,
-        [halves, halves, square, square, (32, N)],
-        [flags, flags, square, sems],
-        velocity, wind, thick, ice, land,
-        far=True, flops=10**8,
-    )
+    alive = (ice * (1 - land)).astype(F32)
+    (edges,) = call(edge_columns, [(32, N)], [square], vel, wind, thick, alive, flops=10**8)
     a, b = call(pack_columns, [(24, N)] * 2, [square], edges, ra, rb)
     ca, cb = neighbours(a, b, "gx")
     send, l, u, r, vsys, sth = call(

time: 74.2 us -> 74.1 us (level)
  local copies, waits for them, and re-layouts: 3.42 us -> 1.62 us
  waiting for transfers between devices: 2.15 us -> 3.08 us
  other arithmetic: 0 us -> 0.88 us
    unnamed x12 -> x8, local copies, waits for them, and re-layouts: 3.42 us -> 0.92 us
    ppermute x4, waiting for transfers between devices: 2.15 us -> 3.08 us  [the longest x2 3.08 us: neighbours(): far = lax.ppermute(b, axis, outer)]
    convert_element_type x0 -> x1, other arithmetic: none -> 0.88 us  [on_device(): alive = (ice * (1 - land)).astype(F32)]
  transfers between devices with their start and end apart: 4 -> 4, of which waited for: 1 -> 1; matrix products, arithmetic and copies ran while one was open for 0% -> 1% of each run, Pallas kernels for 1% -> 0%
where the time goes in v3:
time: 74.1 us; the launch traced here: 73.7 us
  blocking collectives  55.9 us (75%)
  starting transfers between devices  7.74 us (10%)
  Pallas kernels  4.36 us (6%)
  waiting for transfers between devices  3.08 us (4%)
  local copies, waits for them, and re-layouts  1.62 us (2%)
  other arithmetic  0.88 us (1%)
    all_to_all x4, blocking collectives, share(): moved = lax.all_to_all(rows.reshape(K, width, N), axis, 0, 0, tiled=True)  55.9 us
    ppermute x2, starting transfers between devices, neighbours(): near = lax.ppermute(a, axis, inner)  5.05 us
    pallas_call x8, Pallas kernels, call(): pl.pallas_call(kernel, out_shape=shapes, in_specs=[vmem] * len(args), out...  4.36 us
    ppermute x2, waiting for transfers between devices, neighbours(): far = lax.ppermute(b, axis, outer)  3.08 us
    ppermute x2, starting transfers between devices, neighbours(): far = lax.ppermute(b, axis, outer)  2.69 us
  transfers between devices with their start and end apart: 4, of which 1 were waited for; matrix products, arithmetic and copies ran while one was open for 1% of the time, Pallas kernels for 0%

profile of v3, /device:TPU:1, one launch (start us, length us, event | category | flops | bytes accessed | tf_op | source)
XLA Modules:
  0.0 73.7 jit_solution(584248773501297956)
XLA Ops:
  0.0 0.7 fusion
  0.7 0.9 %copy-done = f32[2,128,128]{2,1,0:T(8,128)S(1)} copy-done((f32[2,128,128]{2,1,0:T(8,128)S(1)}, f32[2,128,128]{2,1,0:T(8,128)}, u32[]{:S(2)}) %copy-start) | copy-done | bytes 131096
  1.6 0.0 copy-start.1
  1.6 2.1 %collective-permute-start = (f32[8,128]{1,0:T(8,128)S(1)}, f32[8,128]{1,0:T(8,128)S(1)}, u32[]{:S(2)}, u32[]{:S(2)}) collective-permute-start(f32[8,128]{1,0:T(8,128)S(1)} %get-tuple-element.26), channel_id=1, source_target_pairs={{0,1},{1,0},{2,3},{3,2},{4,5},{5,4},{6,7},{7,6},{8,9},{9,8},{10,11... | collective-permute-start | bytes 12296 | tf_op jit(solution)/shard_map/ppermute | solution.py:502
  3.8 0.8 %collective-permute-start.1 = (f32[8,128]{1,0:T(8,128)S(1)}, f32[8,128]{1,0:T(8,128)S(1)}, u32[]{:S(2)}, u32[]{:S(2)}) collective-permute-start(f32[8,128]{1,0:T(8,128)S(1)} %get-tuple-element.27), channel_id=1, source_target_pairs={{1,2},{2,1},{3,4},{4,3},{5,6},{6,5},{7,8},{8,7},{9,10},{10,9},{11,... | collective-permute-start | bytes 12296 | tf_op jit(solution)/shard_map/ppermute | solution.py:501
  4.5 0.9 %multiply_convert_fusion.alive = f32[128,128]{1,0:T(8,128)S(1)} fusion(s32[128,128]{1,0:T(8,128)} %param.8, s32[128,128]{1,0:T(8,128)} %param.9), kind=kLoop, calls=%fused_computation | loop fusion | flops 49152 | bytes 196608 | tf_op jit(solution)/shard_map/convert_element_type | solution.py:517
  5.4 0.0 copy-done.2
  5.5 0.2 shard_map.56.edges
  5.7 0.0 collective-permute-done.ra
  5.7 0.0 collective-permute-done.1.rb
  5.7 0.1 shard_map.57
  5.8 2.9 %collective-permute-start.2 = (f32[24,128]{1,0:T(8,128)S(1)}, f32[24,128]{1,0:T(8,128)S(1)}, u32[]{:S(2)}, u32[]{:S(2)}) collective-permute-start(f32[24,128]{1,0:T(8,128)S(1)} %get-tuple-element.28), channel_id=1, source_target_pairs={{0,16},{16,0},{32,48},{48,32},{64,80},{80,64},{96,112},{112,96},{1... | collective-permute-start | bytes 36872 | tf_op jit(solution)/shard_map/ppermute | solution.py:502
  8.7 1.9 %collective-permute-start.3 = (f32[24,128]{1,0:T(8,128)S(1)}, f32[24,128]{1,0:T(8,128)S(1)}, u32[]{:S(2)}, u32[]{:S(2)}) collective-permute-start(f32[24,128]{1,0:T(8,128)S(1)} %get-tuple-element.29), channel_id=1, source_target_pairs={{16,32},{32,16},{48,64},{64,48},{80,96},{96,80},{112,128},{128,112... | collective-permute-start | bytes 36872 | tf_op jit(solution)/shard_map/ppermute | solution.py:501
  10.6 0.0 collective-permute-done.2.ca
  10.6 3.1 %collective-permute-done.3.cb = f32[24,128]{1,0:T(8,128)S(1)} collective-permute-done((f32[24,128]{1,0:T(8,128)S(1)}, f32[24,128]{1,0:T(8,128)S(1)}, u32[]{:S(2)}, u32[]{:S(2)}) %collective-permute-start.3) | collective-permute-done | bytes 12320 | tf_op jit(solution)/shard_map/ppermute | solution.py:501
  13.7 1.2 %shard_map.58 = (f32[256,128]{1,0:T(8,128)S(1)}, f32[128,128]{1,0:T(8,128)S(1)}, f32[128,128]{1,0:T(8,128)S(1)}, f32[128,128]{1,0:T(8,128)S(1)}, f32[5,2,128,128...) custom-call(f32[2,128,128]{2,1,0:T(8,128)S(1)} %copy-done.1, f32[2,128,128]{2,1,0:T(8,128)S(1)} %copy-done.2, ...), custom_call_target="tpu_custom_call" | custom-call | tf_op jit(solution)/shard_map/pallas_call | solution.py:487
  14.9 16.7 %all_to_all.20 = f32[16,16,128]{2,1,0:T(8,128)S(1)} all-to-all(f32[16,16,128]{2,1,0:T(8,128)S(1)} %bitcast.12), channel_id=1, replica_groups=mesh['gx'=16,'gy'=16] {'gx'}, dimensions={0} | all-to-all | bytes 262144 | tf_op jit(solution)/shard_map/all_to_all | solution.py:508
  31.6 0.7 %shard_map.59 = (f32[256,128]{1,0:T(8,128)S(1)}, f32[2,128,128]{2,1,0:T(8,128)S(1)}, f32[3,2,128,128]{3,2,1,0:T(8,128)S(1)}) custom-call(f32[256,128]{1,0:T(8,128)S(1)} %bitcast.8, f32[128,128]{1,0:T(8,128)S(1)} %get-tuple-element.31.pl_, f32[128,128]{1,0:T(8,128)S(1)} %get-tuple-element.32.pu_, f32[128,128]{1,0:T(8,128)S(1)} %get-tuple-element.33.pr_, ...), custom_call_target="tpu_custom_call" | custom-call | tf_op jit(solution)/shard_map/pallas_call | solution.py:487
  32.3 18.5 %all_to_all.21 = f32[16,16,128]{2,1,0:T(8,128)S(1)} all-to-all(f32[16,16,128]{2,1,0:T(8,128)S(1)} %bitcast.13), channel_id=1, replica_groups=mesh['gx'=16,'gy'=16] {'gy'}, dimensions={0} | all-to-all | bytes 262144 | tf_op jit(solution)/shard_map/all_to_all | solution.py:508
  50.8 1.0 %shard_map.60 = (f32[128,128]{1,0:T(8,128)S(1)}, f32[128,128]{1,0:T(8,128)S(1)}, f32[128,128]{1,0:T(8,128)S(1)}, f32[128,128]{1,0:T(8,128)S(1)}, f32[5,1,128,128]{3,2,1,0:T(8,128)S(1)}) custom-call(f32[256,128]{1,0:T(8,128)S(1)} %bitcast.9, f32[3,2,128,128]{3,2,1,0:T(8,128)S(1)} %get-tuple-element.36.vp, f32[2,128,128]{2,1,0:T(8,128)S(1)} %get-tuple-element.37.u_new, ...), custom_call_target="tpu_custom_call" | custom-call | tf_op jit(solution)/shard_map/pallas_call | solution.py:487
  51.8 11.5 %all_to_all.22 = f32[16,8,128]{2,1,0:T(8,128)S(1)} all-to-all(f32[16,8,128]{2,1,0:T(8,128)S(1)} %bitcast.14), channel_id=1, replica_groups=mesh['gx'=16,'gy'=16] {'gx'}, dimensions={0} | all-to-all | bytes 131072 | tf_op jit(solution)/shard_map/all_to_all | solution.py:508
  63.3 0.4 shard_map.61
  63.7 9.3 %all_to_all.23 = f32[16,8,128]{2,1,0:T(8,128)S(1)} all-to-all(f32[16,8,128]{2,1,0:T(8,128)S(1)} %bitcast.15), channel_id=1, replica_groups=mesh['gx'=16,'gy'=16] {'gy'}, dimensions={0} | all-to-all | bytes 131072 | tf_op jit(solution)/shard_map/all_to_all | solution.py:508
  73.0 0.7 %shard_map.62 = f32[2,128,128]{2,1,0:T(8,128)} custom-call(f32[128,128]{1,0:T(8,128)S(1)} %bitcast.11, f32[3,128,128]{2,1,0:T(8,128)S(1)} %get-tuple-element.45.vp, f32[128,128]{1,0:T(8,128)S(1)} %get-tuple-element.46.u_new), custom_call_target="tpu_custom_call" | custom-call | tf_op jit(solution)/shard_map/pallas_call | solution.py:487
  (6 shorter events, 0.0 us)
Async XLA Ops:
  0.7 0.9 %copy-start = (f32[2,128,128]{2,1,0:T(8,128)S(1)}, f32[2,128,128]{2,1,0:T(8,128)}, u32[]{:S(2)}) copy-start(f32[2,128,128]{2,1,0:T(8,128)} %vel.5) | copy-start | bytes 393220
  1.6 3.8 %copy-start.2 = (f32[2,128,128]{2,1,0:T(8,128)S(1)}, f32[2,128,128]{2,1,0:T(8,128)}, u32[]{:S(2)}) copy-start(f32[2,128,128]{2,1,0:T(8,128)} %wind.5) | copy-start | bytes 393220
  1.6 3.8 %copy-start.1 = (f32[2,128,128]{2,1,0:T(8,128)S(1)}, f32[2,128,128]{2,1,0:T(8,128)}, u32[]{:S(2)}) copy-start(f32[2,128,128]{2,1,0:T(8,128)} %vel.5) | copy-start | bytes 393220
  1.6 4.0 %collective-permute-start = (f32[8,128]{1,0:T(8,128)S(1)}, f32[8,128]{1,0:T(8,128)S(1)}, u32[]{:S(2)}, u32[]{:S(2)}) collective-permute-start(f32[8,128]{1,0:T(8,128)S(1)} %get-tuple-element.26), channel_id=1, source_target_pairs={{0,1},{1,0},{2,3},{3,2},{4,5},{5,4},{6,7},{7,6},{8,9},{9,8},{10,11... | collective-permute-start | bytes 12296 | tf_op jit(solution)/shard_map/ppermute | solution.py:502
  3.8 1.7 %copy-start.3 = (f32[128,128]{1,0:T(8,128)S(1)}, f32[128,128]{1,0:T(8,128)}, u32[]{:S(2)}) copy-start(f32[128,128]{1,0:T(8,128)} %thick.3) | copy-start | bytes 196612
  3.8 1.9 %collective-permute-start.1 = (f32[8,128]{1,0:T(8,128)S(1)}, f32[8,128]{1,0:T(8,128)S(1)}, u32[]{:S(2)}, u32[]{:S(2)}) collective-permute-start(f32[8,128]{1,0:T(8,128)S(1)} %get-tuple-element.27), channel_id=1, source_target_pairs={{1,2},{2,1},{3,4},{4,3},{5,6},{6,5},{7,8},{8,7},{9,10},{10,9},{11,... | collective-permute-start | bytes 12296 | tf_op jit(solution)/shard_map/ppermute | solution.py:501
  5.8 4.9 %collective-permute-start.2 = (f32[24,128]{1,0:T(8,128)S(1)}, f32[24,128]{1,0:T(8,128)S(1)}, u32[]{:S(2)}, u32[]{:S(2)}) collective-permute-start(f32[24,128]{1,0:T(8,128)S(1)} %get-tuple-element.28), channel_id=1, source_target_pairs={{0,16},{16,0},{32,48},{48,32},{64,80},{80,64},{96,112},{112,96},{1... | collective-permute-start | bytes 36872 | tf_op jit(solution)/shard_map/ppermute | solution.py:502
  8.7 5.0 %collective-permute-start.3 = (f32[24,128]{1,0:T(8,128)S(1)}, f32[24,128]{1,0:T(8,128)S(1)}, u32[]{:S(2)}, u32[]{:S(2)}) collective-permute-start(f32[24,128]{1,0:T(8,128)S(1)} %get-tuple-element.29), channel_id=1, source_target_pairs={{16,32},{32,16},{48,64},{64,48},{80,96},{96,80},{112,128},{128,112... | collective-permute-start | bytes 36872 | tf_op jit(solution)/shard_map/ppermute | solution.py:501

commit v4 on v3

--- a/solution.py
+++ b/solution.py
@@ -45,15 +45,11 @@
     return jnp.where(jnp.broadcast_to(flag, (rows, N)), a, b)
 
 
-def edge_rows(vel, thick_low, thick_high, send_a, send_b):
+def edge_rows(vel, thick):
     even = lax.rem(lax.axis_index("gy"), 2) == 0
-    for k in range(3):
-        first = vel[k, 0:2] if k < 2 else thick_low[...]
-        final = vel[k, N - 2 : N] if k < 2 else thick_high[...]
-        send_a[2 * k : 2 * k + 2] = pick(even, 2, final, first)
-        send_b[2 * k : 2 * k + 2] = pick(even, 2, first, final)
-    send_a[6:8] = jnp.zeros((2, N), F32)
-    send_b[6:8] = jnp.zeros((2, N), F32)
+    fields = jnp.stack([vel[0], vel[1], thick])
+    first, final = fields[:, :2], fields[:, N - 2 :]
+    return jnp.where(even, final, first), jnp.where(even, first, final)
 
 
 def edge_columns(vel, wind, thick, alive, edges, turn):
@@ -81,7 +77,7 @@
 def pack_columns(edges, ra, rb, send_a, send_b, turn):
     turn[...] = jnp.zeros((N, N), F32)
     for k in range(3):
-        above, below = both_ways(ra[2 * k : 2 * k + 2], rb[2 * k : 2 * k + 2], "gy")
+        above, below = both_ways(ra[k], rb[k], "gy")
         turn[4 * k : 4 * k + 2] = below
         turn[4 * k + 2 : 4 * k + 4] = above
     turn[...] = turn[...].T
@@ -312,7 +308,7 @@
             s[t, 0:TOP] = zero
             s[t, TOP + N :] = zero
             s[t, TOP : TOP + N] = own[...] if t == 0 else side_field(mixed, k)
-        above, below = both_ways(ra[2 * k : 2 * k + 2], rb[2 * k : 2 * k + 2], "gy")
+        above, below = both_ways(ra[k], rb[k], "gy")
         s[0, TOP - 2 : TOP] = below
         s[0, TOP + N : TOP + N + 2] = above
         s[1, TOP - 2 : TOP] = turn[4 * k : 4 * k + 2]
@@ -512,7 +508,7 @@
 def on_device(vel, wind, thick, ice, land):
     square, halves, rim = (N, N), (2, N, N), (2, ROWS, N)
     bands, pad, rowed = (2, 4, N + 16, N), (8, N), (3 * K, N)
-    a, b = call(edge_rows, [(8, N)] * 2, [], vel, thick[:2], thick[N - 2 :])
+    a, b = edge_rows(vel, thick)
     ra, rb = neighbours(a, b, "gy")
     alive = (ice * (1 - land)).astype(F32)
     (edges,) = call(edge_columns, [(32, N)], [square], vel, wind, thick, alive, flops=10**8)

time: 74.1 us -> 73.2 us (0.988)
  local copies, waits for them, and re-layouts: 1.62 us -> 0.01 us
  other arithmetic: 0.88 us -> 1.65 us
    unnamed x8, local copies, waits for them, and re-layouts: 0.92 us -> 0.01 us
    select_n x0 -> x2, other arithmetic: none -> 0.8 us  [edge_rows(): return (jnp.where(even, final, first), jnp.where(even, first, final))]
    pallas_call x8 -> x7, Pallas kernels: 4.36 us -> 4.36 us  [call(): pl.pallas_call(kernel, out_shape=shapes, in_specs=[vmem] * len(args), out...]
where the time goes in v4:
time: 73.2 us; the launch traced here: 72.9 us
  blocking collectives  55.9 us (76%)
  starting transfers between devices  7.75 us (11%)
  Pallas kernels  4.36 us (6%)
  waiting for transfers between devices  3.08 us (4%)
  other arithmetic  1.65 us (2%)
    all_to_all x4, blocking collectives, share(): moved = lax.all_to_all(rows.reshape(K, width, N), axis, 0, 0, tiled=True)  55.9 us
    ppermute x2, starting transfers between devices, neighbours(): near = lax.ppermute(a, axis, inner)  5.06 us
    pallas_call x7, Pallas kernels, call(): pl.pallas_call(kernel, out_shape=shapes, in_specs=[vmem] * len(args), out...  4.36 us
    ppermute x2, waiting for transfers between devices, neighbours(): far = lax.ppermute(b, axis, outer)  3.08 us
    ppermute x2, starting transfers between devices, neighbours(): far = lax.ppermute(b, axis, outer)  2.69 us
  transfers between devices with their start and end apart: 4, of which 1 were waited for; matrix products, arithmetic and copies ran while one was open for 1% of the time, Pallas kernels for 0%

profile of v4, /device:TPU:1, one launch (start us, length us, event | category | flops | bytes accessed | tf_op | source)
XLA Modules:
  0.0 72.9 jit_solution(8540427831797685222)
XLA Ops:
  0.0 0.8 %broadcast_select_fusion = (f32[3,2,128]{2,1,0:T(2,128)S(1)}, f32[3,2,128]{2,1,0:T(2,128)S(1)}, f32[3,2,128]{2,1,0:T(2,128)S(1)}) fusion(pred[]{:T(512)S(6)} %eq.3, f32[1,128,128]{2,1,0:T(8,128)} %bitcast.9, f32[2,128,128]{2,1,0:T(8,128)} %vel.3), kind=kLoop, calls=%fused_computation.3 | loop fusion | flops 2304 | bytes 205825 | tf_op jit(solution)/shard_map/jit(_where)/select_n | solution.py:52
  0.8 2.1 %collective-permute-start = (f32[3,2,128]{2,1,0:T(2,128)S(1)}, f32[3,2,128]{2,1,0:T(2,128)S(1)}, u32[]{:S(2)}, u32[]{:S(2)}) collective-permute-start(f32[3,2,128]{2,1,0:T(2,128)S(1)} %broadcast_select_fusion.1), channel_id=1, source_target_pairs={{0,1},{1,0},{2,3},{3,2},{4,5},{5,4},{6,7},{7,6},{8,9},{9,8},{10,11... | collective-permute-start | bytes 9224 | tf_op jit(solution)/shard_map/ppermute | solution.py:498
  2.9 0.8 %collective-permute-start.1 = (f32[3,2,128]{2,1,0:T(2,128)S(1)}, f32[3,2,128]{2,1,0:T(2,128)S(1)}, u32[]{:S(2)}, u32[]{:S(2)}) collective-permute-start(f32[3,2,128]{2,1,0:T(2,128)S(1)} %get-tuple-element.43), channel_id=1, source_target_pairs={{1,2},{2,1},{3,4},{4,3},{5,6},{6,5},{7,8},{8,7},{9,10},{10,9},{11,... | collective-permute-start | bytes 9224 | tf_op jit(solution)/shard_map/ppermute | solution.py:497
  3.7 0.0 copy-done.3
  3.7 0.9 %multiply_convert_fusion.alive = f32[128,128]{1,0:T(8,128)S(1)} fusion(s32[128,128]{1,0:T(8,128)S(1)} %copy-done.3, s32[128,128]{1,0:T(8,128)} %param.9), kind=kLoop, calls=%fused_computation | loop fusion | flops 49152 | bytes 196608 | tf_op jit(solution)/shard_map/convert_element_type | solution.py:513
  4.6 0.0 copy-done.1
  4.6 0.0 copy-done
  4.6 0.2 shard_map.55.edges
  4.8 0.0 collective-permute-done.ra
  4.8 0.0 collective-permute-done.1.rb
  4.8 0.1 shard_map.56
  4.9 2.9 %collective-permute-start.2 = (f32[24,128]{1,0:T(8,128)S(1)}, f32[24,128]{1,0:T(8,128)S(1)}, u32[]{:S(2)}, u32[]{:S(2)}) collective-permute-start(f32[24,128]{1,0:T(8,128)S(1)} %get-tuple-element.24), channel_id=1, source_target_pairs={{0,16},{16,0},{32,48},{48,32},{64,80},{80,64},{96,112},{112,96},{1... | collective-permute-start | bytes 36872 | tf_op jit(solution)/shard_map/ppermute | solution.py:498
  7.9 1.9 %collective-permute-start.3 = (f32[24,128]{1,0:T(8,128)S(1)}, f32[24,128]{1,0:T(8,128)S(1)}, u32[]{:S(2)}, u32[]{:S(2)}) collective-permute-start(f32[24,128]{1,0:T(8,128)S(1)} %get-tuple-element.25), channel_id=1, source_target_pairs={{16,32},{32,16},{48,64},{64,48},{80,96},{96,80},{112,128},{128,112... | collective-permute-start | bytes 36872 | tf_op jit(solution)/shard_map/ppermute | solution.py:497
  9.8 0.0 collective-permute-done.2.ca
  9.8 3.1 %collective-permute-done.3.cb = f32[24,128]{1,0:T(8,128)S(1)} collective-permute-done((f32[24,128]{1,0:T(8,128)S(1)}, f32[24,128]{1,0:T(8,128)S(1)}, u32[]{:S(2)}, u32[]{:S(2)}) %collective-permute-start.3) | collective-permute-done | bytes 12320 | tf_op jit(solution)/shard_map/ppermute | solution.py:497
  12.9 1.2 %shard_map.57 = (f32[256,128]{1,0:T(8,128)S(1)}, f32[128,128]{1,0:T(8,128)S(1)}, f32[128,128]{1,0:T(8,128)S(1)}, f32[128,128]{1,0:T(8,128)S(1)}, f32[5,2,128,128...) custom-call(f32[2,128,128]{2,1,0:T(8,128)S(1)} %copy-done, f32[2,128,128]{2,1,0:T(8,128)S(1)} %copy-done.1, ...), custom_call_target="tpu_custom_call" | custom-call | tf_op jit(solution)/shard_map/pallas_call | solution.py:483
  14.1 16.7 %all_to_all.20 = f32[16,16,128]{2,1,0:T(8,128)S(1)} all-to-all(f32[16,16,128]{2,1,0:T(8,128)S(1)} %bitcast.14), channel_id=1, replica_groups=mesh['gx'=16,'gy'=16] {'gx'}, dimensions={0} | all-to-all | bytes 262144 | tf_op jit(solution)/shard_map/all_to_all | solution.py:504
  30.7 0.7 %shard_map.58 = (f32[256,128]{1,0:T(8,128)S(1)}, f32[2,128,128]{2,1,0:T(8,128)S(1)}, f32[3,2,128,128]{3,2,1,0:T(8,128)S(1)}) custom-call(f32[256,128]{1,0:T(8,128)S(1)} %bitcast.10, f32[128,128]{1,0:T(8,128)S(1)} %get-tuple-element.27.pl_, f32[128,128]{1,0:T(8,128)S(1)} %get-tuple-element.28.pu_, f32[128,128]{1,0:T(8,128)S(1)} %get-tuple-element.29.pr_, ...), custom_call_target="tpu_custom_call" | custom-call | tf_op jit(solution)/shard_map/pallas_call | solution.py:483
  31.5 18.5 %all_to_all.21 = f32[16,16,128]{2,1,0:T(8,128)S(1)} all-to-all(f32[16,16,128]{2,1,0:T(8,128)S(1)} %bitcast.15), channel_id=1, replica_groups=mesh['gx'=16,'gy'=16] {'gy'}, dimensions={0} | all-to-all | bytes 262144 | tf_op jit(solution)/shard_map/all_to_all | solution.py:504
  49.9 1.0 %shard_map.59 = (f32[128,128]{1,0:T(8,128)S(1)}, f32[128,128]{1,0:T(8,128)S(1)}, f32[128,128]{1,0:T(8,128)S(1)}, f32[128,128]{1,0:T(8,128)S(1)}, f32[5,1,128,128]{3,2,1,0:T(8,128)S(1)}) custom-call(f32[256,128]{1,0:T(8,128)S(1)} %bitcast.11, f32[3,2,128,128]{3,2,1,0:T(8,128)S(1)} %get-tuple-element.32.vp, f32[2,128,128]{2,1,0:T(8,128)S(1)} %get-tuple-element.33.u_new, ...), custom_call_target="tpu_custom_call" | custom-call | tf_op jit(solution)/shard_map/pallas_call | solution.py:483
  51.0 11.5 %all_to_all.22 = f32[16,8,128]{2,1,0:T(8,128)S(1)} all-to-all(f32[16,8,128]{2,1,0:T(8,128)S(1)} %bitcast.16), channel_id=1, replica_groups=mesh['gx'=16,'gy'=16] {'gx'}, dimensions={0} | all-to-all | bytes 131072 | tf_op jit(solution)/shard_map/all_to_all | solution.py:504
  62.4 0.4 shard_map.60
  62.8 9.3 %all_to_all.23 = f32[16,8,128]{2,1,0:T(8,128)S(1)} all-to-all(f32[16,8,128]{2,1,0:T(8,128)S(1)} %bitcast.17), channel_id=1, replica_groups=mesh['gx'=16,'gy'=16] {'gy'}, dimensions={0} | all-to-all | bytes 131072 | tf_op jit(solution)/shard_map/all_to_all | solution.py:504
  72.1 0.7 %shard_map.61 = f32[2,128,128]{2,1,0:T(8,128)} custom-call(f32[128,128]{1,0:T(8,128)S(1)} %bitcast.13, f32[3,128,128]{2,1,0:T(8,128)S(1)} %get-tuple-element.41.vp, f32[128,128]{1,0:T(8,128)S(1)} %get-tuple-element.42.u_new), custom_call_target="tpu_custom_call" | custom-call | tf_op jit(solution)/shard_map/pallas_call | solution.py:483
  (6 shorter events, 0.0 us)
Async XLA Ops:
  0.0 3.7 %copy-start.3 = (s32[128,128]{1,0:T(8,128)S(1)}, s32[128,128]{1,0:T(8,128)}, u32[]{:S(2)}) copy-start(s32[128,128]{1,0:T(8,128)} %param.8) | copy-start | bytes 196612
  0.0 4.6 %copy-start.1 = (f32[2,128,128]{2,1,0:T(8,128)S(1)}, f32[2,128,128]{2,1,0:T(8,128)}, u32[]{:S(2)}) copy-start(f32[2,128,128]{2,1,0:T(8,128)} %wind.5) | copy-start | bytes 393220
  0.8 3.8 %copy-start = (f32[2,128,128]{2,1,0:T(8,128)S(1)}, f32[2,128,128]{2,1,0:T(8,128)}, u32[]{:S(2)}) copy-start(f32[2,128,128]{2,1,0:T(8,128)} %vel.3) | copy-start | bytes 393220
  0.8 4.0 %collective-permute-start = (f32[3,2,128]{2,1,0:T(2,128)S(1)}, f32[3,2,128]{2,1,0:T(2,128)S(1)}, u32[]{:S(2)}, u32[]{:S(2)}) collective-permute-start(f32[3,2,128]{2,1,0:T(2,128)S(1)} %broadcast_select_fusion.1), channel_id=1, source_target_pairs={{0,1},{1,0},{2,3},{3,2},{4,5},{5,4},{6,7},{7,6},{8,9},{9,8},{10,11... | collective-permute-start | bytes 9224 | tf_op jit(solution)/shard_map/ppermute | solution.py:498
  2.9 1.7 %copy-start.2 = (f32[128,128]{1,0:T(8,128)S(1)}, f32[128,128]{1,0:T(8,128)}, u32[]{:S(2)}) copy-start(f32[128,128]{1,0:T(8,128)} %thick.3) | copy-start | bytes 196612
  2.9 1.9 %collective-permute-start.1 = (f32[3,2,128]{2,1,0:T(2,128)S(1)}, f32[3,2,128]{2,1,0:T(2,128)S(1)}, u32[]{:S(2)}, u32[]{:S(2)}) collective-permute-start(f32[3,2,128]{2,1,0:T(2,128)S(1)} %get-tuple-element.43), channel_id=1, source_target_pairs={{1,2},{2,1},{3,4},{4,3},{5,6},{6,5},{7,8},{8,7},{9,10},{10,9},{11,... | collective-permute-start | bytes 9224 | tf_op jit(solution)/shard_map/ppermute | solution.py:497
  4.9 4.9 %collective-permute-start.2 = (f32[24,128]{1,0:T(8,128)S(1)}, f32[24,128]{1,0:T(8,128)S(1)}, u32[]{:S(2)}, u32[]{:S(2)}) collective-permute-start(f32[24,128]{1,0:T(8,128)S(1)} %get-tuple-element.24), channel_id=1, source_target_pairs={{0,16},{16,0},{32,48},{48,32},{64,80},{80,64},{96,112},{112,96},{1... | collective-permute-start | bytes 36872 | tf_op jit(solution)/shard_map/ppermute | solution.py:498
  7.9 5.0 %collective-permute-start.3 = (f32[24,128]{1,0:T(8,128)S(1)}, f32[24,128]{1,0:T(8,128)S(1)}, u32[]{:S(2)}, u32[]{:S(2)}) collective-permute-start(f32[24,128]{1,0:T(8,128)S(1)} %get-tuple-element.25), channel_id=1, source_target_pairs={{16,32},{32,16},{48,64},{64,48},{80,96},{96,80},{112,128},{128,112... | collective-permute-start | bytes 36872 | tf_op jit(solution)/shard_map/ppermute | solution.py:497

commit v5 on v4

--- a/solution.py
+++ b/solution.py
@@ -285,12 +285,12 @@
 
 
 def spread(dest, me, common, forward=None, backward=None):
-    width = 8 if forward is None else 16
+    width = dest.shape[0] // K
     for d in range(K):
         at = d * width
         dest[at : at + 8] = common
         if forward is not None:
-            dest[at + 8 : at + 16] = pick(me < d, 8, forward, backward)
+            dest[at + 8 : at + width] = pick(me < d, width - 8, forward[: width - 8], backward[: width - 8])
 
 
 def tile_of(rows, pad):
@@ -369,7 +369,7 @@
 
 def first_v(got, pl_, pu_, pr_, vsys, send, u_new, vp, turn, bands, pad, rowed):
     me = lax.axis_index("gx")
-    before, own, ahead, first, second = solve_pieces(rows_of(got, 16), me, rowed, rows_beside(got, 16, 8, me))
+    before, own, ahead, first, second = solve_pieces(rows_of(got, 11), me, rowed, rows_beside(got, 11, 8, me))
     turn[...] = pr_[...] + pl_[...] * before + pu_[...] * own
     u_new[0] = turn[...].T
     turn[...] = jnp.zeros((N, N), F32)
@@ -501,7 +501,8 @@
 
 def share(rows, axis):
     width = rows.shape[0] // K
-    moved = lax.all_to_all(rows.reshape(K, width, N), axis, 0, 0, tiled=True)
+    inside = (width, N) if width % 8 == 0 else (1, width * N)
+    moved = lax.all_to_all(rows.reshape(K, *inside), axis, 0, 0, tiled=True)
     return moved.reshape(K * width, N)
 
 
@@ -516,7 +517,7 @@
     ca, cb = neighbours(a, b, "gx")
     send, l, u, r, vsys, sth = call(
         first_u,
-        [(K * 16, N), square, square, square, (5,) + halves, rim],
+        [(K * 11, N), square, square, square, (5,) + halves, rim],
         [rim] * 4 + [square, (6, N, N), bands, pad],
         vel, wind, thick, alive, ra, rb, ca, cb,
     )

time: 73.2 us -> 72.4 us (0.989)
  blocking collectives: 55.9 us -> 55.1 us
    all_to_all x4, blocking collectives: 55.9 us -> 55.1 us  [share(): moved = lax.all_to_all(rows.reshape(K, *inside), axis, 0, 0, tiled=True)]
where the time goes in v5:
time: 72.4 us; the launch traced here: 72 us
  blocking collectives  55.1 us (76%)
  starting transfers between devices  7.75 us (11%)
  Pallas kernels  4.36 us (6%)
  waiting for transfers between devices  3.08 us (4%)
  other arithmetic  1.65 us (2%)
    all_to_all x4, blocking collectives, share(): moved = lax.all_to_all(rows.reshape(K, *inside), axis, 0, 0, tiled=True)  55.1 us
    ppermute x2, starting transfers between devices, neighbours(): near = lax.ppermute(a, axis, inner)  5.06 us
    pallas_call x7, Pallas kernels, call(): pl.pallas_call(kernel, out_shape=shapes, in_specs=[vmem] * len(args), out...  4.36 us
    ppermute x2, waiting for transfers between devices, neighbours(): far = lax.ppermute(b, axis, outer)  3.08 us
    ppermute x2, starting transfers between devices, neighbours(): far = lax.ppermute(b, axis, outer)  2.69 us
  transfers between devices with their start and end apart: 4, of which 1 were waited for; matrix products, arithmetic and copies ran while one was open for 1% of the time, Pallas kernels for 0%

profile of v5, /device:TPU:1, one launch (start us, length us, event | category | flops | bytes accessed | tf_op | source)
XLA Modules:
  0.0 72.0 jit_solution(13942667701242674985)
XLA Ops:
  0.0 0.8 %broadcast_select_fusion = (f32[3,2,128]{2,1,0:T(2,128)S(1)}, f32[3,2,128]{2,1,0:T(2,128)S(1)}, f32[3,2,128]{2,1,0:T(2,128)S(1)}) fusion(pred[]{:T(512)S(6)} %eq.3, f32[1,128,128]{2,1,0:T(8,128)} %bitcast.9, f32[2,128,128]{2,1,0:T(8,128)} %vel.3), kind=kLoop, calls=%fused_computation.3 | loop fusion | flops 2304 | bytes 205825 | tf_op jit(solution)/shard_map/jit(_where)/select_n | solution.py:52
  0.8 2.1 %collective-permute-start = (f32[3,2,128]{2,1,0:T(2,128)S(1)}, f32[3,2,128]{2,1,0:T(2,128)S(1)}, u32[]{:S(2)}, u32[]{:S(2)}) collective-permute-start(f32[3,2,128]{2,1,0:T(2,128)S(1)} %broadcast_select_fusion.1), channel_id=1, source_target_pairs={{0,1},{1,0},{2,3},{3,2},{4,5},{5,4},{6,7},{7,6},{8,9},{9,8},{10,11... | collective-permute-start | bytes 9224 | tf_op jit(solution)/shard_map/ppermute | solution.py:498
  2.9 0.8 %collective-permute-start.1 = (f32[3,2,128]{2,1,0:T(2,128)S(1)}, f32[3,2,128]{2,1,0:T(2,128)S(1)}, u32[]{:S(2)}, u32[]{:S(2)}) collective-permute-start(f32[3,2,128]{2,1,0:T(2,128)S(1)} %get-tuple-element.43), channel_id=1, source_target_pairs={{1,2},{2,1},{3,4},{4,3},{5,6},{6,5},{7,8},{8,7},{9,10},{10,9},{11,... | collective-permute-start | bytes 9224 | tf_op jit(solution)/shard_map/ppermute | solution.py:497
  3.7 0.0 copy-done.3
  3.7 0.9 %multiply_convert_fusion.alive = f32[128,128]{1,0:T(8,128)S(1)} fusion(s32[128,128]{1,0:T(8,128)S(1)} %copy-done.3, s32[128,128]{1,0:T(8,128)} %param.9), kind=kLoop, calls=%fused_computation | loop fusion | flops 49152 | bytes 196608 | tf_op jit(solution)/shard_map/convert_element_type | solution.py:514
  4.6 0.0 copy-done.1
  4.6 0.0 copy-done
  4.6 0.2 shard_map.55.edges
  4.8 0.0 collective-permute-done.ra
  4.8 0.0 collective-permute-done.1.rb
  4.8 0.1 shard_map.56
  4.9 2.9 %collective-permute-start.2 = (f32[24,128]{1,0:T(8,128)S(1)}, f32[24,128]{1,0:T(8,128)S(1)}, u32[]{:S(2)}, u32[]{:S(2)}) collective-permute-start(f32[24,128]{1,0:T(8,128)S(1)} %get-tuple-element.24), channel_id=1, source_target_pairs={{0,16},{16,0},{32,48},{48,32},{64,80},{80,64},{96,112},{112,96},{1... | collective-permute-start | bytes 36872 | tf_op jit(solution)/shard_map/ppermute | solution.py:498
  7.9 1.9 %collective-permute-start.3 = (f32[24,128]{1,0:T(8,128)S(1)}, f32[24,128]{1,0:T(8,128)S(1)}, u32[]{:S(2)}, u32[]{:S(2)}) collective-permute-start(f32[24,128]{1,0:T(8,128)S(1)} %get-tuple-element.25), channel_id=1, source_target_pairs={{16,32},{32,16},{48,64},{64,48},{80,96},{96,80},{112,128},{128,112... | collective-permute-start | bytes 36872 | tf_op jit(solution)/shard_map/ppermute | solution.py:497
  9.8 0.0 collective-permute-done.2.ca
  9.8 3.1 %collective-permute-done.3.cb = f32[24,128]{1,0:T(8,128)S(1)} collective-permute-done((f32[24,128]{1,0:T(8,128)S(1)}, f32[24,128]{1,0:T(8,128)S(1)}, u32[]{:S(2)}, u32[]{:S(2)}) %collective-permute-start.3) | collective-permute-done | bytes 12320 | tf_op jit(solution)/shard_map/ppermute | solution.py:497
  12.9 1.2 %shard_map.57 = (f32[176,128]{1,0:T(8,128)S(1)}, f32[128,128]{1,0:T(8,128)S(1)}, f32[128,128]{1,0:T(8,128)S(1)}, f32[128,128]{1,0:T(8,128)S(1)}, f32[5,2,128,128...) custom-call(f32[2,128,128]{2,1,0:T(8,128)S(1)} %copy-done, f32[2,128,128]{2,1,0:T(8,128)S(1)} %copy-done.1, ...), custom_call_target="tpu_custom_call" | custom-call | tf_op jit(solution)/shard_map/pallas_call | solution.py:483
  14.0 16.1 %all_to_all.20 = f32[16,1,1408]{2,1,0:T(1,128)S(1)} all-to-all(f32[16,1,1408]{2,1,0:T(1,128)S(1)} %bitcast.15), channel_id=1, replica_groups=mesh['gx'=16,'gy'=16] {'gx'}, dimensions={0} | all-to-all | bytes 180224 | tf_op jit(solution)/shard_map/all_to_all | solution.py:505
  30.1 0.7 %shard_map.58 = (f32[256,128]{1,0:T(8,128)S(1)}, f32[2,128,128]{2,1,0:T(8,128)S(1)}, f32[3,2,128,128]{3,2,1,0:T(8,128)S(1)}) custom-call(f32[176,128]{1,0:T(8,128)S(1)} %bitcast.11, f32[128,128]{1,0:T(8,128)S(1)} %get-tuple-element.27.pl_, f32[128,128]{1,0:T(8,128)S(1)} %get-tuple-element.28.pu_, f32[128,128]{1,0:T(8,128)S(1)} %get-tuple-element.29.pr_, ...), custom_call_target="tpu_custom_call" | custom-call | tf_op jit(solution)/shard_map/pallas_call | solution.py:483
  30.9 18.4 %all_to_all.21 = f32[16,16,128]{2,1,0:T(8,128)S(1)} all-to-all(f32[16,16,128]{2,1,0:T(8,128)S(1)} %bitcast.14), channel_id=1, replica_groups=mesh['gx'=16,'gy'=16] {'gy'}, dimensions={0} | all-to-all | bytes 262144 | tf_op jit(solution)/shard_map/all_to_all | solution.py:505
  49.2 1.0 %shard_map.59 = (f32[128,128]{1,0:T(8,128)S(1)}, f32[128,128]{1,0:T(8,128)S(1)}, f32[128,128]{1,0:T(8,128)S(1)}, f32[128,128]{1,0:T(8,128)S(1)}, f32[5,1,128,128]{3,2,1,0:T(8,128)S(1)}) custom-call(f32[256,128]{1,0:T(8,128)S(1)} %bitcast.10, f32[3,2,128,128]{3,2,1,0:T(8,128)S(1)} %get-tuple-element.32.vp, f32[2,128,128]{2,1,0:T(8,128)S(1)} %get-tuple-element.33.u_new, ...), custom_call_target="tpu_custom_call" | custom-call | tf_op jit(solution)/shard_map/pallas_call | solution.py:483
  50.3 11.3 %all_to_all.22 = f32[16,8,128]{2,1,0:T(8,128)S(1)} all-to-all(f32[16,8,128]{2,1,0:T(8,128)S(1)} %bitcast.16), channel_id=1, replica_groups=mesh['gx'=16,'gy'=16] {'gx'}, dimensions={0} | all-to-all | bytes 131072 | tf_op jit(solution)/shard_map/all_to_all | solution.py:505
  61.6 0.4 shard_map.60
  62.0 9.3 %all_to_all.23 = f32[16,8,128]{2,1,0:T(8,128)S(1)} all-to-all(f32[16,8,128]{2,1,0:T(8,128)S(1)} %bitcast.17), channel_id=1, replica_groups=mesh['gx'=16,'gy'=16] {'gy'}, dimensions={0} | all-to-all | bytes 131072 | tf_op jit(solution)/shard_map/all_to_all | solution.py:505
  71.3 0.7 %shard_map.61 = f32[2,128,128]{2,1,0:T(8,128)} custom-call(f32[128,128]{1,0:T(8,128)S(1)} %bitcast.13, f32[3,128,128]{2,1,0:T(8,128)S(1)} %get-tuple-element.41.vp, f32[128,128]{1,0:T(8,128)S(1)} %get-tuple-element.42.u_new), custom_call_target="tpu_custom_call" | custom-call | tf_op jit(solution)/shard_map/pallas_call | solution.py:483
  (6 shorter events, 0.0 us)
Async XLA Ops:
  0.0 3.7 %copy-start.3 = (s32[128,128]{1,0:T(8,128)S(1)}, s32[128,128]{1,0:T(8,128)}, u32[]{:S(2)}) copy-start(s32[128,128]{1,0:T(8,128)} %param.8) | copy-start | bytes 196612
  0.0 4.6 %copy-start.1 = (f32[2,128,128]{2,1,0:T(8,128)S(1)}, f32[2,128,128]{2,1,0:T(8,128)}, u32[]{:S(2)}) copy-start(f32[2,128,128]{2,1,0:T(8,128)} %wind.5) | copy-start | bytes 393220
  0.8 3.8 %copy-start = (f32[2,128,128]{2,1,0:T(8,128)S(1)}, f32[2,128,128]{2,1,0:T(8,128)}, u32[]{:S(2)}) copy-start(f32[2,128,128]{2,1,0:T(8,128)} %vel.3) | copy-start | bytes 393220
  0.8 4.0 %collective-permute-start = (f32[3,2,128]{2,1,0:T(2,128)S(1)}, f32[3,2,128]{2,1,0:T(2,128)S(1)}, u32[]{:S(2)}, u32[]{:S(2)}) collective-permute-start(f32[3,2,128]{2,1,0:T(2,128)S(1)} %broadcast_select_fusion.1), channel_id=1, source_target_pairs={{0,1},{1,0},{2,3},{3,2},{4,5},{5,4},{6,7},{7,6},{8,9},{9,8},{10,11... | collective-permute-start | bytes 9224 | tf_op jit(solution)/shard_map/ppermute | solution.py:498
  2.9 1.7 %copy-start.2 = (f32[128,128]{1,0:T(8,128)S(1)}, f32[128,128]{1,0:T(8,128)}, u32[]{:S(2)}) copy-start(f32[128,128]{1,0:T(8,128)} %thick.3) | copy-start | bytes 196612
  2.9 1.9 %collective-permute-start.1 = (f32[3,2,128]{2,1,0:T(2,128)S(1)}, f32[3,2,128]{2,1,0:T(2,128)S(1)}, u32[]{:S(2)}, u32[]{:S(2)}) collective-permute-start(f32[3,2,128]{2,1,0:T(2,128)S(1)} %get-tuple-element.43), channel_id=1, source_target_pairs={{1,2},{2,1},{3,4},{4,3},{5,6},{6,5},{7,8},{8,7},{9,10},{10,9},{11,... | collective-permute-start | bytes 9224 | tf_op jit(solution)/shard_map/ppermute | solution.py:497
  4.9 4.9 %collective-permute-start.2 = (f32[24,128]{1,0:T(8,128)S(1)}, f32[24,128]{1,0:T(8,128)S(1)}, u32[]{:S(2)}, u32[]{:S(2)}) collective-permute-start(f32[24,128]{1,0:T(8,128)S(1)} %get-tuple-element.24), channel_id=1, source_target_pairs={{0,16},{16,0},{32,48},{48,32},{64,80},{80,64},{96,112},{112,96},{1... | collective-permute-start | bytes 36872 | tf_op jit(solution)/shard_map/ppermute | solution.py:498
  7.9 5.0 %collective-permute-start.3 = (f32[24,128]{1,0:T(8,128)S(1)}, f32[24,128]{1,0:T(8,128)S(1)}, u32[]{:S(2)}, u32[]{:S(2)}) collective-permute-start(f32[24,128]{1,0:T(8,128)S(1)} %get-tuple-element.25), channel_id=1, source_target_pairs={{16,32},{32,16},{48,64},{64,48},{80,96},{96,80},{112,128},{128,112... | collective-permute-start | bytes 36872 | tf_op jit(solution)/shard_map/ppermute | solution.py:497
